TPU v7x, 256 devices: a whole 4x4x8 slice. The times are simulated.
256 devices in a mesh: depth: 2 (over x_hi), tx: 16 (over z, core), ty: 8 (over x_lo, y).
Axes of the slice: x: 4 (x_hi: 2, x_lo: 2; x = x_hi * 2 + x_lo), y: 4, z: 8, core: 2. Of those that a mesh axis runs over, the one named last changes fastest.
Arguments:
- down_state: float32 [2, 8, 2, 2, 512, 1024], P('depth', None, None, None, 'tx', 'ty'), may hold values from -6 to 6
- up_state: float32 [2, 8, 2, 2, 512, 1024], P('depth', None, None, None, 'tx', 'ty'), may hold values from -6 to 6
- incident: float32 [8, 2, 2, 512, 1024], P(None, None, None, 'tx', 'ty'), may hold values from -6 to 6
- medium_map: int32 [2, 512, 1024], P('depth', 'tx', 'ty'), may hold values from 0 to 15
- media_table: float32 [16, 16], replicated, may hold values from -0.3 to 0.3
- tap_index: int32 [2, 2], P('depth'), may hold values from 0 to 7, as said below
- kernel_bank: float32 [8, 2, 33], replicated, may hold values from -0.7 to 0.7
Outputs:
- down_final: float32 [2, 8, 2, 2, 512, 1024], P('depth', None, None, None, 'tx', 'ty')
- up_final: float32 [2, 8, 2, 2, 512, 1024], P('depth', None, None, None, 'tx', 'ty')
Inputs may be any that keep to these rules, and one draw needn't show every extreme that they name: `tap_index`: all entries are distinct; 0 and 7 both occur.
All inputs are finite; a program needn't handle non-finite values.
Results may differ from a plain program's by a relative error of at most 0.00011.
Values sent between devices are 32-bit elements; how exact they have to be, the bound alone decides.
No kernel may reach another device: no remote copies, remote signals or barrier semaphores. Data moves between devices by JAX's collectives and lax.ppermute only.
A program may use at most 64 MiB of HBM per device.

v0:
```python
import functools

import jax
import jax.numpy as jnp
from jax import lax
from jax.experimental import pallas as pl
from jax.experimental.pallas import tpu as pltpu
from jax.sharding import PartitionSpec as P

f32 = jnp.float32
bf16 = jnp.bfloat16
VM = pltpu.VMEM
UNITS = 8
TAPS = 33
HALF = 16
ROWS = 32
COLS = 128


def call(body, outs, ins, flops=0, limit=8, scratch=()):
    return pl.pallas_call(
        body,
        out_shape=[jax.ShapeDtypeStruct(s, d) for s, d in outs],
        in_specs=[pl.BlockSpec(memory_space=m) for m in ins],
        out_specs=[pl.BlockSpec(memory_space=VM)] * len(outs),
        scratch_shapes=list(scratch),
        cost_estimate=pl.CostEstimate(flops=flops, bytes_accessed=0, transcendentals=0),
        compiler_params=pltpu.CompilerParams(vmem_limit_bytes=limit * 1024 * 1024),
    )


def split(x):
    hi = x.astype(bf16)
    lo = (x - hi.astype(f32)).astype(bf16)
    return hi, lo


def dot(a, b):
    return jnp.dot(a, b, preferred_element_type=f32)


def section(odd):
    depth = lax.axis_index("depth")
    return 1 - depth if odd else depth


def band(diff, bank, row):
    re = jnp.zeros(diff.shape, f32)
    im = jnp.zeros(diff.shape, f32)
    for k in range(TAPS):
        hit = diff == k
        re = jnp.where(hit, bank[row, k], re)
        im = jnp.where(hit, bank[row + 1, k], im)
    return re, im


def iota(shape, dim):
    return lax.broadcasted_iota(jnp.int32, shape, dim)


def field(o, n):
    return [[o[(n * 2 + p) * 32 : (n * 2 + p) * 32 + 32, c * 128 : c * 128 + 128] for c in range(2)] for p in range(2)]


def jones(m, v):
    out = []
    for q in range(2):
        re = im = None
        for p in range(2):
            a, b = m[q * 2 + p], m[4 + q * 2 + p]
            r = a * v[p][0] - b * v[p][1]
            i = a * v[p][1] + b * v[p][0]
            re, im = (r, i) if re is None else (re + r, im + i)
        out.append((re, im))
    return out


def halves_body(down, up, top, bot):
    def unit(u, _):
        for n, src in enumerate((down, up)):
            for c in range(2):
                for p in range(2):
                    x = src[u, c, p]
                    top[n * UNITS + u, c, p] = x[0:HALF]
                    bot[n * UNITS + u, c, p] = x[HALF:ROWS]
        return 0

    lax.fori_loop(0, UNITS, unit, 0)


def put(pack, lane16, x, first, k):
    shift = (16 * k - first) % 128
    return jnp.where(lane16 == k, pltpu.roll(x, shift, 1) if shift else x, pack)


def edges_body(inc, mmap, low, high):
    lane16 = iota((ROWS, COLS), 1) >> 4
    zero = jnp.zeros((ROWS, COLS), f32)
    for dst, first in ((low, 0), (high, 112)):
        x = mmap[...].astype(f32)
        pack = zero
        for k in range(8):
            pack = put(pack, lane16, x, first, k)
        dst[4] = pack

    def group(g, _):
        for p in range(2):
            for dst, first in ((low, 0), (high, 112)):
                pack = zero
                for n in range(4):
                    for c in range(2):
                        pack = put(pack, lane16, inc[g * 4 + n, c, p], first, n * 2 + c)
                dst[g * 2 + p] = pack
        return 0

    lax.fori_loop(0, UNITS // 4, group, 0)


def quadrants(re, im, row, col):
    quad = row * 2 + col
    return jnp.where(quad == 1, -im, jnp.where(quad == 2, im, re))


def entries(m, table, first, shape):
    hits = [m == e for e in range(16)]
    out = []
    for q in range(first, first + 8):
        v = jnp.zeros(shape, f32)
        for e in range(16):
            v = jnp.where(hits[e], table[e, q], v)
        if q in (0, 3):
            v = v + 0.5
        out.append(v)
    return out


def prep_body(tap_own, tap_other, bank, table, map_own, map_other, amat, wide, bhi, blo, shi, slo, trans, refl):
    depth = lax.axis_index("depth")
    tx, ty = lax.axis_index("tx"), lax.axis_index("ty")
    tx_low, tx_high = tx == 0, tx == lax.axis_size("tx") - 1
    ty_low, ty_high = ty == 0, ty == lax.axis_size("ty") - 1
    for s in range(2):
        mine = depth == s
        k_row = jnp.where(mine, tap_own[0, 0], tap_other[0, 0]) * 2
        k_col = jnp.where(mine, tap_own[0, 1], tap_other[0, 1]) * 2
        i, j = iota((64, 128), 0), iota((64, 128), 1)
        jj = j & 63
        re, im = band(jj - (i & 31), bank, k_row)
        a = quadrants(re, im, i >> 5, j >> 6)
        gone = ((jj < HALF) & tx_low) | ((jj >= 48) & tx_high)
        a = jnp.where(gone, 0.0, a)
        hi, lo = split(a)
        amat[s, 0:64, 0:128] = hi
        amat[s, 0:64, 128:256] = hi
        amat[s, 64:128, 0:128] = lo
        amat[s, 64:128, 128:256] = jnp.zeros_like(lo)

        for r in range(2):
            i, j = iota((64, 192), 0), iota((64, 192), 1)
            col = (j >= 96).astype(jnp.int32)
            jj = j - 96 * col
            re, im = band(jj - i, bank, k_row)
            a = quadrants(re, im, r, col)
            gone = ((jj < 32) & tx_low) | ((jj >= 64) & tx_high)
            hi, lo = split(jnp.where(gone, 0.0, a))
            wide[s, 0, 64 * r : 64 * r + 64] = hi
            wide[s, 1, 64 * r : 64 * r + 64] = lo

        for part in range(2):
            i, j = iota((64, 128), 1), iota((64, 128), 0) + (HALF + 64 * part)
            re, im = band(j - i, bank, k_col)
            (rh, rl), (ih, il) = split(re), split(im)
            for c, (hr, hm, lr, lm) in enumerate(((rh, ih, rl, il), (-ih, rh, -il, rl))):
                rows = pl.ds(c * 128 + 64 * part, 64)
                bhi[s, rows, 0:128] = hr
                bhi[s, rows, 128:256] = hm
                blo[s, rows, 0:128] = lr
                blo[s, rows, 128:256] = lm
        r, i = iota((64, 128), 0), iota((64, 128), 1)
        side = r >> 5
        re, im = band((r & 15) + side * 144 - i, bank, k_col)
        gone = ((side == 0) & ty_low) | ((side == 1) & ty_high)
        re, im = jnp.where(gone, 0.0, re), jnp.where(gone, 0.0, im)
        isim = ((r >> 4) & 1) == 1
        zero = jnp.zeros((64, 128), bf16)
        for n, v in enumerate((jnp.where(isim, -im, re), jnp.where(isim, re, im))):
            hi, lo = split(v)
            cols = pl.ds(n * 128, 128)
            bhi[s, 256:320, cols] = hi
            blo[s, 256:320, cols] = lo
            bhi[s, 320:384, cols] = zero
            blo[s, 320:384, cols] = zero

        m = jnp.where(mine, map_own[...], map_other[...])
        for q, v in enumerate(entries(m, table, 0, (ROWS, COLS))):
            trans[s, q] = v
        for q, v in enumerate(entries(m, table, 8, (ROWS, COLS))):
            refl[s, q] = v if s == 0 else -v

    for part in range(6):
        r, j = iota((64, 128), 0) + 64 * part, iota((64, 128), 1)
        l = (r >> 7) * 16 + (r & 15)
        diff = jnp.where(((r >> 5) & 3) == (j >> 5), l - (j & 15), -1)
        re, im = band(diff, bank, tap_own[0, 1] * 2)
        a = quadrants(re, im, (j >> 4) & 1, (r >> 4) & 1)
        hi, lo = split(a)
        shi[64 * part : 64 * part + 64] = hi
        slo[64 * part : 64 * part + 64] = lo


def strips_body(table, elow, ehigh, trans, refl):
    sign = jnp.where(section(0) == 0, 1.0, -1.0).astype(f32)
    im = ((iota((ROWS, COLS), 1) >> 4) & 1) == 1
    for side, e in enumerate((elow, ehigh)):
        m = (e[4] + 0.5).astype(jnp.int32)
        for dst, first, factor in ((trans, 0, 1.0), (refl, 8, sign)):
            for q, v in enumerate(entries(m, table, first, (ROWS, COLS))):
                v = v * factor
                dst[side, q] = v if q < 4 else jnp.where(im, v, -v)


def taller_body(table, trans, refl, utop, ubot, tall_t, tall_r):
    o = section(1)
    sign = jnp.where(o == 0, 1.0, -1.0).astype(f32)
    for q in range(8):
        tall_t[q, 16:48] = trans[0, q]
        tall_r[q, 16:48] = refl[o, q]
    for dst, x in ((0, utop[32, 16:32]), (48, ubot[32, 0:16])):
        m = (x + 0.5).astype(jnp.int32)
        for q, v in enumerate(entries(m, table, 0, (16, COLS))):
            tall_t[q, dst : dst + 16] = v
        for q, v in enumerate(entries(m, table, 8, (16, COLS))):
            tall_r[q, dst : dst + 16] = v * sign


def stack(rows):
    return jnp.concatenate(
        [jnp.concatenate([r(c, p) for p in range(2)], axis=1) for c in range(2) for r in rows], axis=0
    )


def narrow(lhs, v):
    hi, lo = split(v)
    o = dot(lhs, jnp.concatenate([hi, lo], axis=0))
    return o[0:64] + o[64:128]


def broad(hi, lo, v):
    vh, vl = split(v)
    return dot(hi, vh) + dot(hi, vl) + dot(lo, vh)


def part(o, rows, c, p):
    return o[c * rows : c * rows + rows, p * 128 : p * 128 + 128]


def fields(o, rows):
    return [[part(o, rows, c, p) for c in range(2)] for p in range(2)]


EDGES = ((0, 16), (112, 96))


def row_body(amat, top, bot, htop, hbot, w, low, high):
    lane16 = iota((ROWS, COLS), 1) >> 4
    lhs = amat[section(0)]

    def group(g, _):
        packs = [[[jnp.zeros((ROWS, COLS), f32) for _ in range(2)] for _ in range(2)] for _ in range(2)]
        for n in range(4):
            u = g * 4 + n
            o = narrow(lhs, stack([lambda c, p, x=x: x[u, c, p] for x in (htop, top, bot, hbot)]))
            for c in range(2):
                for p in range(2):
                    x = part(o, 32, c, p)
                    w[u, c, p] = x
                    for side in range(2):
                        for far in range(2):
                            packs[side][far][p] = put(packs[side][far][p], lane16, x, EDGES[side][far], n * 2 + c)
        for p in range(2):
            for far in range(2):
                low[far, g, p] = packs[0][far][p]
                high[far, g, p] = packs[1][far][p]
        return 0

    lax.fori_loop(0, 2 * UNITS // 4, group, 0)


def columns(w, hlow, hhigh, g, bh, bl):
    lane = iota((ROWS, COLS), 1)
    rows = []
    for n in range(4):
        for p in range(2):
            a, b = hlow(g, p), hhigh(g, p)
            a = pltpu.roll(a, 128 - 32 * n, 1) if n else a
            b = pltpu.roll(b, (160 - 32 * n) % 128, 1) if n != 1 else b
            u = g * 4 + n
            rows.append(jnp.concatenate([w[u, 0, p], w[u, 1, p], jnp.where(lane < 32, a, b)], axis=1))
    hi, lo = split(jnp.concatenate(rows, axis=0))
    return dot(hi, bh) + dot(lo, bh) + dot(hi, bl)


def inc_column_body(bhi, blo, inc, elow, ehigh, map_other, out):
    bh, bl = bhi[0], blo[0]

    def group(g, _):
        o = columns(inc, lambda g, p: elow[g * 2 + p], lambda g, p: ehigh[g * 2 + p], g, bh, bl)
        for n in range(4):
            f = field(o, n)
            for c in range(2):
                for p in range(2):
                    out[(g * 4 + n) * 4 + c * 2 + p] = f[p][c]
        return 0

    lax.fori_loop(0, UNITS // 4, group, 0)
    out[32] = map_other[...].astype(f32)


def inc_row_body(wide, tall_t, x, utop, ubot, const):
    hi, lo = wide[0, 0], wide[0, 1]

    def unit(u, _):
        o = broad(hi, lo, stack([lambda c, p, y=y: y[u * 4 + c * 2 + p] for y in (utop, x, ubot)]))
        a = jones([tall_t[q] for q in range(8)], fields(o, 64))
        for p in range(2):
            for c in range(2):
                const[u, c, p] = a[p][c]
        return 0

    lax.fori_loop(0, UNITS, unit, 0)


def column_body(first, bhi, blo, shi, slo, trans, refl, strans, srefl, const, w, low, high, hlow, hhigh, *rest):
    out, mid, slow, shigh = rest[-4:]
    outs = rest[:-4] + (out,)
    d = section(0)
    gate = jnp.where(d == 0, 1.0, 0.0).astype(f32)
    sh, sl = shi[...], slo[...]
    im = ((iota((ROWS, COLS), 1) >> 4) & 1) == 1

    def swapped(x):
        return jnp.where(im, pltpu.roll(x, 16, 1), pltpu.roll(x, 112, 1))

    def group_of(which, g):
        if not first:
            return g
        return (d if which == 0 else 1 - d) * 2 + g

    def strip_group(g, _):
        rows = []
        for side in range(2):
            for which in range(2 if first else 1):
                k = group_of(which, g)
                for p in range(2):
                    if side == 0:
                        x = (hlow[1, k, p], hlow[0, k, p], low[0, k, p])
                    else:
                        x = (high[0, k, p], hhigh[0, k, p], hhigh[1, k, p])
                    rows.append(jnp.concatenate(x, axis=1))
        hi, lo = split(jnp.concatenate(rows, axis=0))
        o = dot(hi, sh) + dot(lo, sh) + dot(hi, sl)
        n = 0
        for side in range(2):
            mats = (strans, srefl) if first else (srefl,)
            acc = [jnp.zeros((ROWS, COLS), f32)] * 2
            for m in mats:
                for p in range(2):
                    x = o[n * 32 : n * 32 + 32]
                    n += 1
                    y = swapped(x)
                    for q in range(2):
                        acc[q] = acc[q] + m[side, q * 2 + p] * x + m[side, 4 + q * 2 + p] * y
            for q in range(2):
                dst, halo = ((slow, hlow), (shigh, hhigh))[side]
                dst[g, q] = acc[q] if first else acc[q] + gate * halo[2, g, q]
        return 0

    lax.fori_loop(0, UNITS // 4, strip_group, 0)
    bh, bl = bhi[d], blo[d]

    def main_group(g, _):
        os = [
            columns(w, lambda g, p: hlow[0, g, p], lambda g, p: hhigh[0, g, p], group_of(k, g), bh, bl)
            for k in range(2 if first else 1)
        ]
        for n in range(4):
            u = g * 4 + n
            b = jones([refl[d, q] for q in range(8)], field(os[-1], n))
            if first:
                a = jones([trans[d, q] for q in range(8)], field(os[0], n))
            for p in range(2):
                for c in range(2):
                    extra = a[p][c] if first else gate * const[u, c, p, 16:48]
                    mid[u, c, p] = b[p][c] + extra
        return 0

    lax.fori_loop(0, UNITS // 4, main_group, 0)
    ch, cl = bhi[1 - d], blo[1 - d]

    def next_group(g, _):
        o = columns(mid, lambda g, p: slow[g, p], lambda g, p: shigh[g, p], g, ch, cl)
        for n in range(4):
            f = field(o, n)
            for c in range(2):
                for p in range(2):
                    if first:
                        out[g * 4 + n, c, p] = f[p][c]
                    else:
                        outs[0][g * 4 + n, c, p] = f[p][c][0:16]
                        outs[1][g * 4 + n, c, p] = f[p][c][16:32]
        return 0

    lax.fori_loop(0, UNITS // 4, next_group, 0)


def second_body(amat, wide, tall_r, const, x, htop, hbot, w, low, high):
    lane16 = iota((ROWS, COLS), 1) >> 4
    d, o = section(0), section(1)
    gate = jnp.where(o == 0, 1.0, 0.0).astype(f32)
    lhs = amat[d]
    hi, lo = wide[o, 0], wide[o, 1]

    def group(g, _):
        packs = [[[jnp.zeros((ROWS, COLS), f32) for _ in range(2)] for _ in range(3)] for _ in range(2)]
        for n in range(4):
            u = g * 4 + n
            v = broad(hi, lo, stack([lambda c, p, y=y: y[u, c, p] for y in (htop, x, hbot)]))
            b = jones([tall_r[q] for q in range(8)], fields(v, 64))
            v = narrow(lhs, stack([lambda c, p: b[p][c] + gate * const[u, c, p]]))
            for c in range(2):
                for p in range(2):
                    y = part(v, 32, c, p)
                    w[u, c, p] = y
                    z = const[u, c, p, 16:48]
                    for side in range(2):
                        for far in range(3):
                            packs[side][far][p] = put(
                                packs[side][far][p],
                                lane16,
                                z if far == 2 else y,
                                EDGES[side][far % 2],
                                n * 2 + c,
                            )
        for p in range(2):
            for far in range(3):
                low[far, g, p] = packs[0][far][p]
                high[far, g, p] = packs[1][far][p]
        return 0

    lax.fori_loop(0, UNITS // 4, group, 0)


def last_body(amat, refl, const, inc, top, bot, htop, hbot, down, up):
    o = section(1)
    gate = jnp.where(o == 0, 1.0, 0.0).astype(f32)
    top_section = lax.axis_index("depth") == 0
    lhs = amat[o]

    def unit(u, _):
        v = narrow(lhs, stack([lambda c, p, x=x: x[u, c, p] for x in (htop, top, bot, hbot)]))
        b = jones([refl[o, q] for q in range(8)], fields(v, 32))
        for p in range(2):
            for c in range(2):
                y = b[p][c] + gate * const[u, c, p, 16:48]
                down[u, c, p] = jnp.where(top_section, inc[u, c, p], y)
                up[u, c, p] = jnp.where(top_section, y, 0.0)
        return 0

    lax.fori_loop(0, UNITS, unit, 0)


def both_ways(low, high, axis):
    n = lax.axis_size(axis)
    up = [(i, (i + 1) % n) for i in range(n)]
    back = [(t, s) for s, t in up]
    return lax.ppermute(high, axis, up), lax.ppermute(low, axis, back)


def on_device(down_state, up_state, incident, medium_map, media_table, tap_index, kernel_bank):
    SM = pltpu.SMEM

    def half(n):
        return (n, 2, 2, HALF, COLS), f32

    def full(n):
        return (n, 2, 2, ROWS, COLS), f32

    def packs(kinds, n):
        return (kinds, n // 4, 2, ROWS, COLS), f32

    def planes(*n):
        return n + (ROWS, COLS), f32

    top, bot = call(halves_body, [half(16)] * 2, [VM] * 2, flops=1 << 20)(down_state[0], up_state[0])
    htop, hbot = both_ways(top, bot, "tx")

    note = jnp.concatenate([medium_map[0], jnp.pad(tap_index, ((0, 7), (0, COLS - 2)))], axis=0)
    note = lax.ppermute(note, "depth", [(0, 1), (1, 0)])
    map_other = note[0:ROWS]
    elow, ehigh = both_ways(
        *call(edges_body, [planes(5)] * 2, [VM] * 2, flops=1 << 20)(incident, medium_map[0]), "ty"
    )
    amat, wide, bhi, blo, shi, slo, trans, refl = call(
        prep_body,
        [
            ((2, 128, 256), bf16),
            ((2, 2, 128, 192), bf16),
            ((2, 384, 256), bf16),
            ((2, 384, 256), bf16),
            ((384, 128), bf16),
            ((384, 128), bf16),
            planes(2, 8),
            planes(2, 8),
        ],
        [SM] * 4 + [VM] * 2,
        flops=1 << 27,
    )(
        tap_index,
        note[ROWS : ROWS + 1, 0:2],
        kernel_bank.reshape(-1, TAPS),
        media_table,
        medium_map[0],
        map_other,
    )
    strans, srefl = call(strips_body, [planes(2, 8)] * 2, [SM] + [VM] * 2, flops=1 << 25)(
        media_table, elow, ehigh
    )
    inc_cols = call(inc_column_body, [planes(33)], [VM] * 6, flops=1 << 26)(
        bhi, blo, incident, elow, ehigh, map_other
    )[0]

    htop, hbot, inc_cols = lax.optimization_barrier((htop, hbot, inc_cols))
    w, low, high = call(row_body, [full(16)] + [packs(2, 16)] * 2, [VM] * 5, flops=1 << 27)(
        amat, top, bot, htop, hbot
    )
    low, high, inc_cols = lax.optimization_barrier((low, high, inc_cols))
    hlow, hhigh = both_ways(low, high, "ty")
    utop, ubot = both_ways(inc_cols, inc_cols, "tx")

    def two_ticks(first, outs, *args):
        scratch = [VM(*full(UNITS)), VM((2, 2, ROWS, COLS), f32), VM((2, 2, ROWS, COLS), f32)]
        return call(functools.partial(column_body, first), outs, [VM] * len(args), flops=1 << 27, scratch=scratch)(*args)

    mats = (bhi, blo, shi, slo, trans, refl, strans, srefl)
    x = two_ticks(True, [full(UNITS)], *mats, trans, w, low, high, hlow, hhigh)[0]
    htop, hbot = both_ways(x, x, "tx")
    tall = ((8, 64, COLS), f32)
    tall_t, tall_r = call(taller_body, [tall] * 2, [SM] + [VM] * 4, flops=1 << 25)(
        media_table, trans, refl, utop, ubot
    )
    const = call(inc_row_body, [((UNITS, 2, 2, 64, COLS), f32)], [VM] * 5, flops=1 << 26)(
        wide, tall_t, inc_cols, utop, ubot
    )[0]
    w, low, high = call(second_body, [full(UNITS)] + [packs(3, UNITS)] * 2, [VM] * 7, flops=1 << 27)(
        amat, wide, tall_r, const, x, htop, hbot
    )
    hlow, hhigh = both_ways(low, high, "ty")
    top, bot = two_ticks(False, [half(UNITS)] * 2, *mats, const, w, low, high, hlow, hhigh)
    htop, hbot = both_ways(top, bot, "tx")
    down, up = call(last_body, [full(UNITS)] * 2, [VM] * 8, flops=1 << 27)(
        amat, refl, const, incident, top, bot, htop, hbot
    )
    return down[None], up[None]


def solution(mesh):
    in_specs = (
        P("depth", None, None, None, "tx", "ty"),
        P("depth", None, None, None, "tx", "ty"),
        P(None, None, None, "tx", "ty"),
        P("depth", "tx", "ty"),
        P(),
        P("depth", None),
        P(),
    )
    out_specs = (P("depth", None, None, None, "tx", "ty"), P("depth", None, None, None, "tx", "ty"))
    return jax.shard_map(
        on_device, mesh=mesh, in_specs=in_specs, out_specs=out_specs, check_vma=False
    )
```

profile of v0, /device:TPU:24, one launch (start us, length us, event | category | flops | bytes accessed | tf_op | source)
XLA Modules:
  0.0 71.8 jit_solution(14043960398065060469)
XLA Ops:
  0.6 1.0 %copy-done.1 = f32[1,8,2,2,32,128]{5,4,3,2,1,0:T(8,128)S(1)} copy-done((f32[1,8,2,2,32,128]{5,4,3,2,1,0:T(8,128)S(1)}, f32[1,8,2,2,32,128]{5,4,3,2,1,0:T(8,128)}, u32[]{:S(2)}) %copy-start.1) | copy-done | bytes 524312
  1.7 1.0 %copy-done.2 = f32[1,8,2,2,32,128]{5,4,3,2,1,0:T(8,128)S(1)} copy-done((f32[1,8,2,2,32,128]{5,4,3,2,1,0:T(8,128)S(1)}, f32[1,8,2,2,32,128]{5,4,3,2,1,0:T(8,128)}, u32[]{:S(2)}) %copy-start.2) | copy-done | bytes 524312
  2.8 5.3 %collective-permute-start.2 = (f32[16,2,2,16,128]{4,3,2,1,0:T(8,128)S(1)}, f32[16,2,2,16,128]{4,3,2,1,0:T(8,128)S(1)}, u32[]{:S(2)}, u32[]{:S(2)}) collective-permute-start(f32[16,2,2,16,128]{4,3,2,1,0:T(8,128)S(1)} %get-tuple-element.38.top), channel_id=1, source_target_pairs={{8,0},{16,8},{24,16},{32,24},{40,32},{48,40},{56,48},{64,56},{72,6... | collective-permute-start | bytes 1572872 | tf_op jit(solution)/shard_map/ppermute | solution.py:476
  8.7 1.2 %collective-permute-start.3 = (f32[5,32,128]{2,1,0:T(8,128)S(1)}, f32[5,32,128]{2,1,0:T(8,128)S(1)}, u32[]{:S(2)}, u32[]{:S(2)}) collective-permute-start(f32[5,32,128]{2,1,0:T(8,128)S(1)} %get-tuple-element.42), channel_id=1, source_target_pairs={{0,1},{1,2},{2,3},{3,4},{4,5},{5,6},{6,7},{7,0},{8,9},{9,10},{10,1... | collective-permute-start | bytes 245768 | tf_op jit(solution)/shard_map/ppermute | solution.py:476
  10.8 3.1 %collective-permute-start = (s32[40,128]{1,0:T(8,128)S(1)}, s32[40,128]{1,0:T(8,128)S(1)}, u32[]{:S(2)}, u32[]{:S(2)}) collective-permute-start(s32[40,128]{1,0:T(8,128)S(1)} %pad_add_fusion), channel_id=1, source_target_pairs={{0,128},{128,0},{1,129},{129,1},{2,130},{130,2},{3,131},{131,3},{4... | collective-permute-start | bytes 61448 | tf_op jit(solution)/shard_map/ppermute | solution.py:498
  13.9 2.3 %collective-permute-done = s32[40,128]{1,0:T(8,128)S(1)} collective-permute-done((s32[40,128]{1,0:T(8,128)S(1)}, s32[40,128]{1,0:T(8,128)S(1)}, u32[]{:S(2)}, u32[]{:S(2)}) %collective-permute-start) | collective-permute-done | bytes 20512 | tf_op jit(solution)/shard_map/ppermute | solution.py:498
  16.9 4.4 %shard_map.86 = (bf16[2,128,256]{2,1,0:T(8,128)(2,1)S(1)}, bf16[2,2,128,192]{3,2,1,0:T(8,128)(2,1)S(1)}, bf16[2,384,256]{2,1,0:T(8,128)(2,1)S(1)}, bf16[2,384,25...) custom-call(s32[1,2]{1,0:T(1,128)S(1)} %copy-done.5, ...), custom_call_target="tpu_custom_call" | custom-call | flops 134217728 | tf_op jit(solution)/shard_map/pallas_call | solution.py:503
  22.2 2.0 %shard_map.90 = (f32[16,2,2,32,128]{4,3,2,1,0:T(8,128)S(1)}, f32[2,4,2,32,128]{4,3,2,1,0:T(8,128)S(1)}, f32[2,4,2,32,128]{4,3,2,1,0:T(8,128)S(1)}) custom-call(bf16[2,128,256]{2,1,0:T(8,128)(2,1)S(1)} %get-tuple-element.34.amat, f32[16,2,2,16,128]{4,3,2,1,0:T(8,128)S(1)} %get-tuple-element.38.top, f32[16,2,2,16,128]{4,3,2,1,0:T(8,128)S(1)} %get-tuple-element.39.bot, ...), custom_call_target="tpu_custom_call" | custom-call | flops 134217728 | tf_op jit(solution)/shard_map/pallas_call | solution.py:533
  24.2 3.3 %collective-permute-start.7 = (f32[2,4,2,32,128]{4,3,2,1,0:T(8,128)S(1)}, f32[2,4,2,32,128]{4,3,2,1,0:T(8,128)S(1)}, u32[]{:S(2)}, u32[]{:S(2)}) collective-permute-start(f32[2,4,2,32,128]{4,3,2,1,0:T(8,128)S(1)} %get-tuple-element.58.high), channel_id=1, source_target_pairs={{0,1},{1,2},{2,3},{3,4},{4,5},{5,6},{6,7},{7,0},{8,9},{9,10},{10,1... | collective-permute-start | bytes 786440 | tf_op jit(solution)/shard_map/ppermute | solution.py:476
  27.6 3.0 %collective-permute-start.6 = (f32[33,32,128]{2,1,0:T(8,128)S(1)}, f32[33,32,128]{2,1,0:T(8,128)S(1)}, u32[]{:S(2)}, u32[]{:S(2)}) collective-permute-start(f32[33,32,128]{2,1,0:T(8,128)S(1)} %shard_map.89.x), channel_id=1, source_target_pairs={{8,0},{16,8},{24,16},{32,24},{40,32},{48,40},{56,48},{64,56},{72,6... | collective-permute-start | bytes 1622024 | tf_op jit(solution)/shard_map/ppermute | solution.py:476
  30.5 1.3 %shard_map.93 = (f32[2,8,32,128]{3,2,1,0:T(8,128)S(1)}, f32[2,8,32,128]{3,2,1,0:T(8,128)S(1)}) custom-call(f32[16,16]{1,0:T(8,128)S(1)} %copy-done.4, f32[5,32,128]{2,1,0:T(8,128)S(1)} %collective-permute-done.3.elow, f32[5,32,128]{2,1,0:T(8,128)S(1)} %collective-permute-done.4.ehigh), custom_call_target="tpu_custom_call" | custom-call | flops 33554432 | tf_op jit(solution)/shard_map/pallas_call | solution.py:525
  31.8 4.2 %collective-permute-done.8.hhigh = f32[2,4,2,32,128]{4,3,2,1,0:T(8,128)S(1)} collective-permute-done((f32[2,4,2,32,128]{4,3,2,1,0:T(8,128)S(1)}, f32[2,4,2,32,128]{4,3,2,1,0:T(8,128)S(1)}, u32[]{:S(2)}, u32[]{:S(2)}) %collective-permute-start.8) | collective-permute-done | bytes 262176 | tf_op jit(solution)/shard_map/ppermute | solution.py:476
  36.1 3.1 %shard_map.94.x = f32[8,2,2,32,128]{4,3,2,1,0:T(8,128)S(1)} custom-call(bf16[2,384,256]{2,1,0:T(8,128)(2,1)S(1)} %get-tuple-element.40.bhi, bf16[2,384,256]{2,1,0:T(8,128)(2,1)S(1)} %get-tuple-element.41.blo, bf16[384,128]{1,0:T(8,128)(2,1)S(1)} %get-tuple-element.51.shi, bf16[384,128]{1,0:T(8,128)(2,1)S(1)} %get-tuple-element.52.slo, ...), custom_call_target="tpu_custom_call" | custom-call | flops 134217728 | tf_op jit(solution)/shard_map/pallas_call | solution.py:542
  39.2 2.9 %collective-permute-start.10 = (f32[8,2,2,32,128]{4,3,2,1,0:T(8,128)S(1)}, f32[8,2,2,32,128]{4,3,2,1,0:T(8,128)S(1)}, u32[]{:S(2)}, u32[]{:S(2)}) collective-permute-start(f32[8,2,2,32,128]{4,3,2,1,0:T(8,128)S(1)} %shard_map.94.x), channel_id=1, source_target_pairs={{8,0},{16,8},{24,16},{32,24},{40,32},{48,40},{56,48},{64,56},{72,6... | collective-permute-start | bytes 1572872 | tf_op jit(solution)/shard_map/ppermute | solution.py:476
  43.1 1.9 %shard_map.92.const = f32[8,2,2,64,128]{4,3,2,1,0:T(8,128)S(1)} custom-call(bf16[2,2,128,192]{3,2,1,0:T(8,128)(2,1)S(1)} %get-tuple-element.36.wide, f32[8,64,128]{2,1,0:T(8,128)S(1)} %get-tuple-element.50.tall_t, f32[33,32,128]{2,1,0:T(8,128)S(1)} %shard_map.89.x, f32[33,32,128]{2,1,0:T(8,128)S(1)} %collective-permute-done.5.utop, ...), custom_call_target="tpu_custom_call" | custom-call | flops 67108864 | tf_op jit(solution)/shard_map/pallas_call | solution.py:551
  45.0 4.0 %collective-permute-done.9.htop = f32[8,2,2,32,128]{4,3,2,1,0:T(8,128)S(1)} collective-permute-done((f32[8,2,2,32,128]{4,3,2,1,0:T(8,128)S(1)}, f32[8,2,2,32,128]{4,3,2,1,0:T(8,128)S(1)}, u32[]{:S(2)}, u32[]{:S(2)}) %collective-permute-start.9) | collective-permute-done | bytes 524320 | tf_op jit(solution)/shard_map/ppermute | solution.py:476
  49.0 2.9 %shard_map.95 = (f32[8,2,2,32,128]{4,3,2,1,0:T(8,128)S(1)}, f32[3,2,2,32,128]{4,3,2,1,0:T(8,128)S(1)}, f32[3,2,2,32,128]{4,3,2,1,0:T(8,128)S(1)}) custom-call(bf16[2,128,256]{2,1,0:T(8,128)(2,1)S(1)} %get-tuple-element.34.amat, bf16[2,2,128,192]{3,2,1,0:T(8,128)(2,1)S(1)} %get-tuple-element.36.wide, f32[8,64,128]{2,1,0:T(8,128)S(1)} %get-tuple-element.55.tall_r, ...), custom_call_target="tpu_custom_call" | custom-call | flops 134217728 | tf_op jit(solution)/shard_map/pallas_call | solution.py:554
  52.0 2.0 %collective-permute-start.12 = (f32[3,2,2,32,128]{4,3,2,1,0:T(8,128)S(1)}, f32[3,2,2,32,128]{4,3,2,1,0:T(8,128)S(1)}, u32[]{:S(2)}, u32[]{:S(2)}) collective-permute-start(f32[3,2,2,32,128]{4,3,2,1,0:T(8,128)S(1)} %get-tuple-element.60.low), channel_id=1, source_target_pairs={{1,0},{2,1},{3,2},{4,3},{5,4},{6,5},{7,6},{0,7},{9,8},{10,9},{11,1... | collective-permute-start | bytes 589832 | tf_op jit(solution)/shard_map/ppermute | solution.py:476
  54.0 3.6 %collective-permute-done.11.hlow = f32[3,2,2,32,128]{4,3,2,1,0:T(8,128)S(1)} collective-permute-done((f32[3,2,2,32,128]{4,3,2,1,0:T(8,128)S(1)}, f32[3,2,2,32,128]{4,3,2,1,0:T(8,128)S(1)}, u32[]{:S(2)}, u32[]{:S(2)}) %collective-permute-start.11) | collective-permute-done | bytes 196640 | tf_op jit(solution)/shard_map/ppermute | solution.py:476
  57.7 2.2 %collective-permute-done.12.hhigh = f32[3,2,2,32,128]{4,3,2,1,0:T(8,128)S(1)} collective-permute-done((f32[3,2,2,32,128]{4,3,2,1,0:T(8,128)S(1)}, f32[3,2,2,32,128]{4,3,2,1,0:T(8,128)S(1)}, u32[]{:S(2)}, u32[]{:S(2)}) %collective-permute-start.12) | collective-permute-done | bytes 196640 | tf_op jit(solution)/shard_map/ppermute | solution.py:476
  59.9 2.5 %shard_map.96 = (f32[8,2,2,16,128]{4,3,2,1,0:T(8,128)S(1)}, f32[8,2,2,16,128]{4,3,2,1,0:T(8,128)S(1)}) custom-call(bf16[2,384,256]{2,1,0:T(8,128)(2,1)S(1)} %get-tuple-element.40.bhi, bf16[2,384,256]{2,1,0:T(8,128)(2,1)S(1)} %get-tuple-element.41.blo, bf16[384,128]{1,0:T(8,128)(2,1)S(1)} %get-tuple-element.51.shi, ...), custom_call_target="tpu_custom_call" | custom-call | flops 134217728 | tf_op jit(solution)/shard_map/pallas_call | solution.py:542
  62.4 2.9 %collective-permute-start.14 = (f32[8,2,2,16,128]{4,3,2,1,0:T(8,128)S(1)}, f32[8,2,2,16,128]{4,3,2,1,0:T(8,128)S(1)}, u32[]{:S(2)}, u32[]{:S(2)}) collective-permute-start(f32[8,2,2,16,128]{4,3,2,1,0:T(8,128)S(1)} %get-tuple-element.62.top), channel_id=1, source_target_pairs={{8,0},{16,8},{24,16},{32,24},{40,32},{48,40},{56,48},{64,56},{72,6... | collective-permute-start | bytes 786440 | tf_op jit(solution)/shard_map/ppermute | solution.py:476
  65.3 4.1 %collective-permute-done.13.htop = f32[8,2,2,16,128]{4,3,2,1,0:T(8,128)S(1)} collective-permute-done((f32[8,2,2,16,128]{4,3,2,1,0:T(8,128)S(1)}, f32[8,2,2,16,128]{4,3,2,1,0:T(8,128)S(1)}, u32[]{:S(2)}, u32[]{:S(2)}) %collective-permute-start.13) | collective-permute-done | bytes 262176 | tf_op jit(solution)/shard_map/ppermute | solution.py:476
  69.4 2.5 %shard_map.97 = (f32[8,2,2,32,128]{4,3,2,1,0:T(8,128)}, f32[8,2,2,32,128]{4,3,2,1,0:T(8,128)}) custom-call(bf16[2,128,256]{2,1,0:T(8,128)(2,1)S(1)} %get-tuple-element.34.amat, f32[2,8,32,128]{3,2,1,0:T(8,128)S(1)} %get-tuple-element.35.refl, f32[8,2,2,64,128]{4,3,2,1,0:T(8,128)S(1)} %shard_map.92.const, f32[8,2,2,32,128]{4,3,2,1,0:T(8,128)S(1)} %copy-done, ...), custom_call_target="tpu_custom_call" | custom-call | flops 134217728 | tf_op jit(solution)/shard_map/pallas_call | solution.py:560
  (35 shorter events, 4.2 us)
Async XLA Ops:
  0.6 1.0 %copy-start.1 = (f32[1,8,2,2,32,128]{5,4,3,2,1,0:T(8,128)S(1)}, f32[1,8,2,2,32,128]{5,4,3,2,1,0:T(8,128)}, u32[]{:S(2)}) copy-start(f32[1,8,2,2,32,128]{5,4,3,2,1,0:T(8,128)} %param.7) | copy-start | bytes 1572868
  1.7 1.0 %copy-start.2 = (f32[1,8,2,2,32,128]{5,4,3,2,1,0:T(8,128)S(1)}, f32[1,8,2,2,32,128]{5,4,3,2,1,0:T(8,128)}, u32[]{:S(2)}) copy-start(f32[1,8,2,2,32,128]{5,4,3,2,1,0:T(8,128)} %param.8) | copy-start | bytes 1572868
  2.7 5.4 %copy-start = (f32[8,2,2,32,128]{4,3,2,1,0:T(8,128)S(1)}, f32[8,2,2,32,128]{4,3,2,1,0:T(8,128)}, u32[]{:S(2)}) copy-start(f32[8,2,2,32,128]{4,3,2,1,0:T(8,128)} %inc.5) | copy-start | bytes 1572868
  2.7 5.4 %copy-start.3 = (s32[1,32,128]{2,1,0:T(8,128)S(1)}, s32[1,32,128]{2,1,0:T(8,128)}, u32[]{:S(2)}) copy-start(s32[1,32,128]{2,1,0:T(8,128)} %param.10) | copy-start | bytes 49156
  2.8 19.4 %collective-permute-start.1 = (f32[16,2,2,16,128]{4,3,2,1,0:T(8,128)S(1)}, f32[16,2,2,16,128]{4,3,2,1,0:T(8,128)S(1)}, u32[]{:S(2)}, u32[]{:S(2)}) collective-permute-start(f32[16,2,2,16,128]{4,3,2,1,0:T(8,128)S(1)} %get-tuple-element.39.bot), channel_id=1, source_target_pairs={{0,8},{8,16},{16,24},{24,32},{32,40},{40,48},{48,56},{56,64},{64,7... | collective-permute-start | bytes 1572872 | tf_op jit(solution)/shard_map/ppermute | solution.py:476
  2.8 19.4 %collective-permute-start.2 = (f32[16,2,2,16,128]{4,3,2,1,0:T(8,128)S(1)}, f32[16,2,2,16,128]{4,3,2,1,0:T(8,128)S(1)}, u32[]{:S(2)}, u32[]{:S(2)}) collective-permute-start(f32[16,2,2,16,128]{4,3,2,1,0:T(8,128)S(1)} %get-tuple-element.38.top), channel_id=1, source_target_pairs={{8,0},{16,8},{24,16},{32,24},{40,32},{48,40},{56,48},{64,56},{72,6... | collective-permute-start | bytes 1572872 | tf_op jit(solution)/shard_map/ppermute | solution.py:476
  8.6 2.1 %copy-start.5 = (s32[1,2]{1,0:T(1,128)S(1)}, s32[1,2]{1,0:T(1,128)}, u32[]{:S(2)}) copy-start(s32[1,2]{1,0:T(1,128)} %tap_own.1) | copy-start | bytes 28
  8.7 12.7 %collective-permute-start.3 = (f32[5,32,128]{2,1,0:T(8,128)S(1)}, f32[5,32,128]{2,1,0:T(8,128)S(1)}, u32[]{:S(2)}, u32[]{:S(2)}) collective-permute-start(f32[5,32,128]{2,1,0:T(8,128)S(1)} %get-tuple-element.42), channel_id=1, source_target_pairs={{0,1},{1,2},{2,3},{3,4},{4,5},{5,6},{6,7},{7,0},{8,9},{9,10},{10,1... | collective-permute-start | bytes 245768 | tf_op jit(solution)/shard_map/ppermute | solution.py:476
  9.9 11.4 %collective-permute-start.4 = (f32[5,32,128]{2,1,0:T(8,128)S(1)}, f32[5,32,128]{2,1,0:T(8,128)S(1)}, u32[]{:S(2)}, u32[]{:S(2)}) collective-permute-start(f32[5,32,128]{2,1,0:T(8,128)S(1)} %get-tuple-element.43), channel_id=1, source_target_pairs={{1,0},{2,1},{3,2},{4,3},{5,4},{6,5},{7,6},{0,7},{9,8},{10,9},{11,1... | collective-permute-start | bytes 245768 | tf_op jit(solution)/shard_map/ppermute | solution.py:476
  10.8 5.4 %collective-permute-start = (s32[40,128]{1,0:T(8,128)S(1)}, s32[40,128]{1,0:T(8,128)S(1)}, u32[]{:S(2)}, u32[]{:S(2)}) collective-permute-start(s32[40,128]{1,0:T(8,128)S(1)} %pad_add_fusion), channel_id=1, source_target_pairs={{0,128},{128,0},{1,129},{129,1},{2,130},{130,2},{3,131},{131,3},{4... | collective-permute-start | bytes 61448 | tf_op jit(solution)/shard_map/ppermute | solution.py:498
  16.1 0.7 copy-start.4
  16.1 0.7 copy-start.6
  24.2 7.6 %collective-permute-start.7 = (f32[2,4,2,32,128]{4,3,2,1,0:T(8,128)S(1)}, f32[2,4,2,32,128]{4,3,2,1,0:T(8,128)S(1)}, u32[]{:S(2)}, u32[]{:S(2)}) collective-permute-start(f32[2,4,2,32,128]{4,3,2,1,0:T(8,128)S(1)} %get-tuple-element.58.high), channel_id=1, source_target_pairs={{0,1},{1,2},{2,3},{3,4},{4,5},{5,6},{6,7},{7,0},{8,9},{9,10},{10,1... | collective-permute-start | bytes 786440 | tf_op jit(solution)/shard_map/ppermute | solution.py:476
  27.6 8.5 %collective-permute-start.8 = (f32[2,4,2,32,128]{4,3,2,1,0:T(8,128)S(1)}, f32[2,4,2,32,128]{4,3,2,1,0:T(8,128)S(1)}, u32[]{:S(2)}, u32[]{:S(2)}) collective-permute-start(f32[2,4,2,32,128]{4,3,2,1,0:T(8,128)S(1)} %get-tuple-element.57.low), channel_id=1, source_target_pairs={{1,0},{2,1},{3,2},{4,3},{5,4},{6,5},{7,6},{0,7},{9,8},{10,9},{11,1... | collective-permute-start | bytes 786440 | tf_op jit(solution)/shard_map/ppermute | solution.py:476
  27.6 14.6 %collective-permute-start.5 = (f32[33,32,128]{2,1,0:T(8,128)S(1)}, f32[33,32,128]{2,1,0:T(8,128)S(1)}, u32[]{:S(2)}, u32[]{:S(2)}) collective-permute-start(f32[33,32,128]{2,1,0:T(8,128)S(1)} %shard_map.89.x), channel_id=1, source_target_pairs={{0,8},{8,16},{16,24},{24,32},{32,40},{40,48},{48,56},{56,64},{64,7... | collective-permute-start | bytes 1622024 | tf_op jit(solution)/shard_map/ppermute | solution.py:476
  27.6 14.6 %collective-permute-start.6 = (f32[33,32,128]{2,1,0:T(8,128)S(1)}, f32[33,32,128]{2,1,0:T(8,128)S(1)}, u32[]{:S(2)}, u32[]{:S(2)}) collective-permute-start(f32[33,32,128]{2,1,0:T(8,128)S(1)} %shard_map.89.x), channel_id=1, source_target_pairs={{8,0},{16,8},{24,16},{32,24},{40,32},{48,40},{56,48},{64,56},{72,6... | collective-permute-start | bytes 1622024 | tf_op jit(solution)/shard_map/ppermute | solution.py:476
  39.2 9.8 %collective-permute-start.9 = (f32[8,2,2,32,128]{4,3,2,1,0:T(8,128)S(1)}, f32[8,2,2,32,128]{4,3,2,1,0:T(8,128)S(1)}, u32[]{:S(2)}, u32[]{:S(2)}) collective-permute-start(f32[8,2,2,32,128]{4,3,2,1,0:T(8,128)S(1)} %shard_map.94.x), channel_id=1, source_target_pairs={{0,8},{8,16},{16,24},{24,32},{32,40},{40,48},{48,56},{56,64},{64,7... | collective-permute-start | bytes 1572872 | tf_op jit(solution)/shard_map/ppermute | solution.py:476
  39.2 9.8 %collective-permute-start.10 = (f32[8,2,2,32,128]{4,3,2,1,0:T(8,128)S(1)}, f32[8,2,2,32,128]{4,3,2,1,0:T(8,128)S(1)}, u32[]{:S(2)}, u32[]{:S(2)}) collective-permute-start(f32[8,2,2,32,128]{4,3,2,1,0:T(8,128)S(1)} %shard_map.94.x), channel_id=1, source_target_pairs={{8,0},{16,8},{24,16},{32,24},{40,32},{48,40},{56,48},{64,56},{72,6... | collective-permute-start | bytes 1572872 | tf_op jit(solution)/shard_map/ppermute | solution.py:476
  51.9 5.7 %collective-permute-start.11 = (f32[3,2,2,32,128]{4,3,2,1,0:T(8,128)S(1)}, f32[3,2,2,32,128]{4,3,2,1,0:T(8,128)S(1)}, u32[]{:S(2)}, u32[]{:S(2)}) collective-permute-start(f32[3,2,2,32,128]{4,3,2,1,0:T(8,128)S(1)} %get-tuple-element.61.high), channel_id=1, source_target_pairs={{0,1},{1,2},{2,3},{3,4},{4,5},{5,6},{6,7},{7,0},{8,9},{9,10},{10,1... | collective-permute-start | bytes 589832 | tf_op jit(solution)/shard_map/ppermute | solution.py:476
  52.0 7.9 %collective-permute-start.12 = (f32[3,2,2,32,128]{4,3,2,1,0:T(8,128)S(1)}, f32[3,2,2,32,128]{4,3,2,1,0:T(8,128)S(1)}, u32[]{:S(2)}, u32[]{:S(2)}) collective-permute-start(f32[3,2,2,32,128]{4,3,2,1,0:T(8,128)S(1)} %get-tuple-element.60.low), channel_id=1, source_target_pairs={{1,0},{2,1},{3,2},{4,3},{5,4},{6,5},{7,6},{0,7},{9,8},{10,9},{11,1... | collective-permute-start | bytes 589832 | tf_op jit(solution)/shard_map/ppermute | solution.py:476
  62.3 7.0 %collective-permute-start.13 = (f32[8,2,2,16,128]{4,3,2,1,0:T(8,128)S(1)}, f32[8,2,2,16,128]{4,3,2,1,0:T(8,128)S(1)}, u32[]{:S(2)}, u32[]{:S(2)}) collective-permute-start(f32[8,2,2,16,128]{4,3,2,1,0:T(8,128)S(1)} %get-tuple-element.63.bot), channel_id=1, source_target_pairs={{0,8},{8,16},{16,24},{24,32},{32,40},{40,48},{48,56},{56,64},{64,7... | collective-permute-start | bytes 786440 | tf_op jit(solution)/shard_map/ppermute | solution.py:476
  62.4 7.0 %collective-permute-start.14 = (f32[8,2,2,16,128]{4,3,2,1,0:T(8,128)S(1)}, f32[8,2,2,16,128]{4,3,2,1,0:T(8,128)S(1)}, u32[]{:S(2)}, u32[]{:S(2)}) collective-permute-start(f32[8,2,2,16,128]{4,3,2,1,0:T(8,128)S(1)} %get-tuple-element.62.top), channel_id=1, source_target_pairs={{8,0},{16,8},{24,16},{32,24},{40,32},{48,40},{56,48},{64,56},{72,6... | collective-permute-start | bytes 786440 | tf_op jit(solution)/shard_map/ppermute | solution.py:476
where the time goes:
time: 73.2 us; the launch traced here: 71.8 us
  starting transfers between devices  24.9 us (34%)
  Pallas kernels  23 us (31%)
  waiting for transfers between devices  20.4 us (28%)
  local copies, waits for them, and re-layouts  2.8 us (4%)
  between operations  0.82 us (1%)
    ppermute x14, starting transfers between devices, both_ways(): return (lax.ppermute(high, axis, up), lax.ppermute(low, axis, back))  21.7 us
    ppermute x14, waiting for transfers between devices, both_ways(): return (lax.ppermute(high, axis, up), lax.ppermute(low, axis, back))  18.1 us
    pallas_call x2, Pallas kernels, two_ticks(): call(functools.partial(column_body, first), outs, [VM] * len(args), flops...  5.58 us
    pallas_call x1, Pallas kernels, on_device(): call(prep_body, [((2, 128, 256), bf16), ((2, 2, 128, 192), bf16), ((2, 38...  4.45 us
    ppermute x1, starting transfers between devices, on_device(): note = lax.ppermute(note, 'depth', [(0, 1), (1, 0)])  3.11 us
    pallas_call x1, Pallas kernels, on_device(): call(second_body, [full(UNITS)] + [packs(3, UNITS)] * 2, [VM] * 7, flops=...  2.9 us
    unnamed x14, local copies, waits for them, and re-layouts  2.8 us
    pallas_call x1, Pallas kernels, on_device(): call(last_body, [full(UNITS)] * 2, [VM] * 8, flops=1 << 27)  2.46 us
  transfers between devices with their start and end apart: 15, of which 6 were waited for; matrix products, arithmetic and copies ran while one was open for 0% of the time, Pallas kernels for 18%

commit v1 on v0

--- a/solution.py
+++ b/solution.py
@@ -17,12 +17,12 @@
 COLS = 128
 
 
-def call(body, outs, ins, flops=0, limit=8, scratch=()):
+def call(body, outs, ins, flops=0, limit=8, scratch=(), home=VM):
     return pl.pallas_call(
         body,
         out_shape=[jax.ShapeDtypeStruct(s, d) for s, d in outs],
         in_specs=[pl.BlockSpec(memory_space=m) for m in ins],
-        out_specs=[pl.BlockSpec(memory_space=VM)] * len(outs),
+        out_specs=[pl.BlockSpec(memory_space=home)] * len(outs),
         scratch_shapes=list(scratch),
         cost_estimate=pl.CostEstimate(flops=flops, bytes_accessed=0, transcendentals=0),
         compiler_params=pltpu.CompilerParams(vmem_limit_bytes=limit * 1024 * 1024),
@@ -134,82 +134,97 @@
     return out
 
 
-def prep_body(tap_own, tap_other, bank, table, map_own, map_other, amat, wide, bhi, blo, shi, slo, trans, refl):
-    depth = lax.axis_index("depth")
+def tables(slot, tap, bank, table, m, sign, amat, bhi, blo, trans, refl):
     tx, ty = lax.axis_index("tx"), lax.axis_index("ty")
     tx_low, tx_high = tx == 0, tx == lax.axis_size("tx") - 1
     ty_low, ty_high = ty == 0, ty == lax.axis_size("ty") - 1
-    for s in range(2):
-        mine = depth == s
-        k_row = jnp.where(mine, tap_own[0, 0], tap_other[0, 0]) * 2
-        k_col = jnp.where(mine, tap_own[0, 1], tap_other[0, 1]) * 2
-        i, j = iota((64, 128), 0), iota((64, 128), 1)
-        jj = j & 63
-        re, im = band(jj - (i & 31), bank, k_row)
-        a = quadrants(re, im, i >> 5, j >> 6)
-        gone = ((jj < HALF) & tx_low) | ((jj >= 48) & tx_high)
-        a = jnp.where(gone, 0.0, a)
-        hi, lo = split(a)
-        amat[s, 0:64, 0:128] = hi
-        amat[s, 0:64, 128:256] = hi
-        amat[s, 64:128, 0:128] = lo
-        amat[s, 64:128, 128:256] = jnp.zeros_like(lo)
-
-        for r in range(2):
-            i, j = iota((64, 192), 0), iota((64, 192), 1)
-            col = (j >= 96).astype(jnp.int32)
-            jj = j - 96 * col
-            re, im = band(jj - i, bank, k_row)
-            a = quadrants(re, im, r, col)
-            gone = ((jj < 32) & tx_low) | ((jj >= 64) & tx_high)
-            hi, lo = split(jnp.where(gone, 0.0, a))
-            wide[s, 0, 64 * r : 64 * r + 64] = hi
-            wide[s, 1, 64 * r : 64 * r + 64] = lo
-
-        for part in range(2):
-            i, j = iota((64, 128), 1), iota((64, 128), 0) + (HALF + 64 * part)
-            re, im = band(j - i, bank, k_col)
-            (rh, rl), (ih, il) = split(re), split(im)
-            for c, (hr, hm, lr, lm) in enumerate(((rh, ih, rl, il), (-ih, rh, -il, rl))):
-                rows = pl.ds(c * 128 + 64 * part, 64)
-                bhi[s, rows, 0:128] = hr
-                bhi[s, rows, 128:256] = hm
-                blo[s, rows, 0:128] = lr
-                blo[s, rows, 128:256] = lm
-        r, i = iota((64, 128), 0), iota((64, 128), 1)
-        side = r >> 5
-        re, im = band((r & 15) + side * 144 - i, bank, k_col)
-        gone = ((side == 0) & ty_low) | ((side == 1) & ty_high)
-        re, im = jnp.where(gone, 0.0, re), jnp.where(gone, 0.0, im)
-        isim = ((r >> 4) & 1) == 1
-        zero = jnp.zeros((64, 128), bf16)
-        for n, v in enumerate((jnp.where(isim, -im, re), jnp.where(isim, re, im))):
-            hi, lo = split(v)
-            cols = pl.ds(n * 128, 128)
-            bhi[s, 256:320, cols] = hi
-            blo[s, 256:320, cols] = lo
-            bhi[s, 320:384, cols] = zero
-            blo[s, 320:384, cols] = zero
-
-        m = jnp.where(mine, map_own[...], map_other[...])
-        for q, v in enumerate(entries(m, table, 0, (ROWS, COLS))):
-            trans[s, q] = v
-        for q, v in enumerate(entries(m, table, 8, (ROWS, COLS))):
-            refl[s, q] = v if s == 0 else -v
-
+    k_row, k_col = tap[0, 0] * 2, tap[0, 1] * 2
+    i, j = iota((64, 128), 0), iota((64, 128), 1)
+    jj = j & 63
+    re, im = band(jj - (i & 31), bank, k_row)
+    a = quadrants(re, im, i >> 5, j >> 6)
+    gone = ((jj < HALF) & tx_low) | ((jj >= 48) & tx_high)
+    a = jnp.where(gone, 0.0, a)
+    hi, lo = split(a)
+    amat[slot, 0:64, 0:128] = hi
+    amat[slot, 0:64, 128:256] = hi
+    amat[slot, 64:128, 0:128] = lo
+    amat[slot, 64:128, 128:256] = jnp.zeros_like(lo)
+
+    for part in range(2):
+        i, j = iota((64, 128), 1), iota((64, 128), 0) + (HALF + 64 * part)
+        re, im = band(j - i, bank, k_col)
+        (rh, rl), (ih, il) = split(re), split(im)
+        for c, (hr, hm, lr, lm) in enumerate(((rh, ih, rl, il), (-ih, rh, -il, rl))):
+            rows = pl.ds(c * 128 + 64 * part, 64)
+            bhi[slot, rows, 0:128] = hr
+            bhi[slot, rows, 128:256] = hm
+            blo[slot, rows, 0:128] = lr
+            blo[slot, rows, 128:256] = lm
+    r, i = iota((64, 128), 0), iota((64, 128), 1)
+    side = r >> 5
+    re, im = band((r & 15) + side * 144 - i, bank, k_col)
+    gone = ((side == 0) & ty_low) | ((side == 1) & ty_high)
+    re, im = jnp.where(gone, 0.0, re), jnp.where(gone, 0.0, im)
+    isim = ((r >> 4) & 1) == 1
+    zero = jnp.zeros((64, 128), bf16)
+    for n, v in enumerate((jnp.where(isim, -im, re), jnp.where(isim, re, im))):
+        hi, lo = split(v)
+        cols = pl.ds(n * 128, 128)
+        bhi[slot, 256:320, cols] = hi
+        blo[slot, 256:320, cols] = lo
+        bhi[slot, 320:384, cols] = zero
+        blo[slot, 320:384, cols] = zero
+
+    for q, v in enumerate(entries(m, table, 0, (ROWS, COLS))):
+        trans[slot, q] = v
+    for q, v in enumerate(entries(m, table, 8, (ROWS, COLS))):
+        refl[slot, q] = v * sign
+
+
+def sign_of(sec):
+    return jnp.where(sec == 0, 1.0, -1.0).astype(f32)
+
+
+def own_body(tap, bank, table, mmap, amat, bhi, blo, trans, refl, shi, slo):
+    tables(0, tap, bank, table, mmap[...], sign_of(section(0)), amat, bhi, blo, trans, refl)
     for part in range(6):
         r, j = iota((64, 128), 0) + 64 * part, iota((64, 128), 1)
         l = (r >> 7) * 16 + (r & 15)
         diff = jnp.where(((r >> 5) & 3) == (j >> 5), l - (j & 15), -1)
-        re, im = band(diff, bank, tap_own[0, 1] * 2)
+        re, im = band(diff, bank, tap[0, 1] * 2)
         a = quadrants(re, im, (j >> 4) & 1, (r >> 4) & 1)
         hi, lo = split(a)
         shi[64 * part : 64 * part + 64] = hi
         slo[64 * part : 64 * part + 64] = lo
 
 
+def other_body(tap, bank, table, mmap, *refs):
+    own, both = refs[:5], refs[5:]
+    o = section(1)
+    for x, y in zip(own, both):
+        y[1 - o] = x[0]
+    tables(o, tap, bank, table, mmap[...], sign_of(o), *both)
+
+
+def wide_body(tap_own, tap_other, bank, x, wide):
+    depth, tx = lax.axis_index("depth"), lax.axis_index("tx")
+    tx_low, tx_high = tx == 0, tx == lax.axis_size("tx") - 1
+    for s in range(2):
+        k_row = jnp.where(depth == s, tap_own[0, 0], tap_other[0, 0]) * 2
+        i, j = iota((64, 96), 0), iota((64, 96), 1)
+        re, im = band(j - i, bank, k_row)
+        gone = ((j < 32) & tx_low) | ((j >= 64) & tx_high)
+        re, im = jnp.where(gone, 0.0, re), jnp.where(gone, 0.0, im)
+        for r in range(2):
+            row = (re, -im) if r == 0 else (im, re)
+            hi, lo = split(jnp.concatenate(row, axis=1))
+            wide[s, 0, 64 * r : 64 * r + 64] = hi
+            wide[s, 1, 64 * r : 64 * r + 64] = lo
+
+
 def strips_body(table, elow, ehigh, trans, refl):
-    sign = jnp.where(section(0) == 0, 1.0, -1.0).astype(f32)
+    sign = sign_of(section(0))
     im = ((iota((ROWS, COLS), 1) >> 4) & 1) == 1
     for side, e in enumerate((elow, ehigh)):
         m = (e[4] + 0.5).astype(jnp.int32)
@@ -221,7 +236,7 @@
 
 def taller_body(table, trans, refl, utop, ubot, tall_t, tall_r):
     o = section(1)
-    sign = jnp.where(o == 0, 1.0, -1.0).astype(f32)
+    sign = sign_of(o)
     for q in range(8):
         tall_t[q, 16:48] = trans[0, q]
         tall_r[q, 16:48] = refl[o, q]
@@ -263,7 +278,7 @@
 
 def row_body(amat, top, bot, htop, hbot, w, low, high):
     lane16 = iota((ROWS, COLS), 1) >> 4
-    lhs = amat[section(0)]
+    lhs = amat[0]
 
     def group(g, _):
         packs = [[[jnp.zeros((ROWS, COLS), f32) for _ in range(2)] for _ in range(2)] for _ in range(2)]
@@ -319,15 +334,16 @@
 def inc_row_body(wide, tall_t, x, utop, ubot, const):
     hi, lo = wide[0, 0], wide[0, 1]
 
-    def unit(u, _):
-        o = broad(hi, lo, stack([lambda c, p, y=y: y[u * 4 + c * 2 + p] for y in (utop, x, ubot)]))
-        a = jones([tall_t[q] for q in range(8)], fields(o, 64))
-        for p in range(2):
-            for c in range(2):
-                const[u, c, p] = a[p][c]
-        return 0
-
-    lax.fori_loop(0, UNITS, unit, 0)
+    def group(g, _):
+        for u in [g * 4 + n for n in range(4)]:
+            o = broad(hi, lo, stack([lambda c, p, y=y: y[u * 4 + c * 2 + p] for y in (utop, x, ubot)]))
+            a = jones([tall_t[q] for q in range(8)], fields(o, 64))
+            for p in range(2):
+                for c in range(2):
+                    const[u, c, p] = a[p][c]
+        return 0
+
+    lax.fori_loop(0, UNITS // 4, group, 0)
 
 
 def column_body(first, bhi, blo, shi, slo, trans, refl, strans, srefl, const, w, low, high, hlow, hhigh, *rest):
@@ -450,23 +466,27 @@
     lax.fori_loop(0, UNITS // 4, group, 0)
 
 
-def last_body(amat, refl, const, inc, top, bot, htop, hbot, down, up):
+def last_body(amat, refl, const, inc, top, bot, htop, hbot, down, up, vdown, vup, sems):
     o = section(1)
     gate = jnp.where(o == 0, 1.0, 0.0).astype(f32)
     top_section = lax.axis_index("depth") == 0
     lhs = amat[o]
-
-    def unit(u, _):
-        v = narrow(lhs, stack([lambda c, p, x=x: x[u, c, p] for x in (htop, top, bot, hbot)]))
-        b = jones([refl[o, q] for q in range(8)], fields(v, 32))
-        for p in range(2):
-            for c in range(2):
-                y = b[p][c] + gate * const[u, c, p, 16:48]
-                down[u, c, p] = jnp.where(top_section, inc[u, c, p], y)
-                up[u, c, p] = jnp.where(top_section, y, 0.0)
-        return 0
-
-    lax.fori_loop(0, UNITS, unit, 0)
+    copies = []
+    for g in range(UNITS // 2):
+        for u in (g * 2, g * 2 + 1):
+            v = narrow(lhs, stack([lambda c, p, x=x: x[u, c, p] for x in (htop, top, bot, hbot)]))
+            b = jones([refl[o, q] for q in range(8)], fields(v, 32))
+            for p in range(2):
+                for c in range(2):
+                    y = b[p][c] + gate * const[u, c, p, 16:48]
+                    vdown[u, c, p] = jnp.where(top_section, inc[u, c, p], y)
+                    vup[u, c, p] = jnp.where(top_section, y, 0.0)
+        for n, (src, dst) in enumerate(((vdown, down), (vup, up))):
+            copy = pltpu.make_async_copy(src.at[pl.ds(g * 2, 2)], dst.at[pl.ds(g * 2, 2)], sems.at[2 * g + n])
+            copy.start()
+            copies.append(copy)
+    for copy in copies:
+        copy.wait()
 
 
 def both_ways(low, high, axis):
@@ -492,50 +512,37 @@
         return n + (ROWS, COLS), f32
 
     top, bot = call(halves_body, [half(16)] * 2, [VM] * 2, flops=1 << 20)(down_state[0], up_state[0])
+    bank = kernel_bank.reshape(-1, TAPS)
     htop, hbot = both_ways(top, bot, "tx")
-
+    elow, ehigh = both_ways(
+        *call(edges_body, [planes(5)] * 2, [VM] * 2, flops=1 << 20)(incident, medium_map[0]), "ty"
+    )
     note = jnp.concatenate([medium_map[0], jnp.pad(tap_index, ((0, 7), (0, COLS - 2)))], axis=0)
     note = lax.ppermute(note, "depth", [(0, 1), (1, 0)])
-    map_other = note[0:ROWS]
-    elow, ehigh = both_ways(
-        *call(edges_body, [planes(5)] * 2, [VM] * 2, flops=1 << 20)(incident, medium_map[0]), "ty"
-    )
-    amat, wide, bhi, blo, shi, slo, trans, refl = call(
-        prep_body,
-        [
-            ((2, 128, 256), bf16),
-            ((2, 2, 128, 192), bf16),
-            ((2, 384, 256), bf16),
-            ((2, 384, 256), bf16),
-            ((384, 128), bf16),
-            ((384, 128), bf16),
-            planes(2, 8),
-            planes(2, 8),
-        ],
-        [SM] * 4 + [VM] * 2,
-        flops=1 << 27,
-    )(
-        tap_index,
-        note[ROWS : ROWS + 1, 0:2],
-        kernel_bank.reshape(-1, TAPS),
-        media_table,
-        medium_map[0],
-        map_other,
-    )
-    strans, srefl = call(strips_body, [planes(2, 8)] * 2, [SM] + [VM] * 2, flops=1 << 25)(
-        media_table, elow, ehigh
+
+    def lookups(n):
+        return [((n, 128, 256), bf16)] + [((n, 384, 256), bf16)] * 2 + [planes(n, 8)] * 2
+
+    *own, shi, slo = call(own_body, lookups(1) + [((384, 128), bf16)] * 2, [SM] * 3 + [VM], flops=1 << 27)(
+        tap_index, bank, media_table, medium_map[0]
+    )
+    htop, hbot, elow, ehigh, note = lax.optimization_barrier((htop, hbot, elow, ehigh, note))
+    w, low, high = call(row_body, [full(16)] + [packs(2, 16)] * 2, [VM] * 5, flops=1 << 27)(
+        own[0], top, bot, htop, hbot
+    )
+    low, high, note, elow, ehigh = lax.optimization_barrier((low, high, note, elow, ehigh))
+    hlow, hhigh = both_ways(low, high, "ty")
+    map_other, tap_other = note[0:ROWS], note[ROWS : ROWS + 1, 0:2]
+    amat, bhi, blo, trans, refl = call(other_body, lookups(2), [SM] * 3 + [VM] * 6, flops=1 << 26)(
+        tap_other, bank, media_table, map_other, *own
     )
     inc_cols = call(inc_column_body, [planes(33)], [VM] * 6, flops=1 << 26)(
         bhi, blo, incident, elow, ehigh, map_other
     )[0]
-
-    htop, hbot, inc_cols = lax.optimization_barrier((htop, hbot, inc_cols))
-    w, low, high = call(row_body, [full(16)] + [packs(2, 16)] * 2, [VM] * 5, flops=1 << 27)(
-        amat, top, bot, htop, hbot
-    )
-    low, high, inc_cols = lax.optimization_barrier((low, high, inc_cols))
-    hlow, hhigh = both_ways(low, high, "ty")
     utop, ubot = both_ways(inc_cols, inc_cols, "tx")
+    strans, srefl = call(strips_body, [planes(2, 8)] * 2, [SM] + [VM] * 2, flops=1 << 25)(
+        media_table, elow, ehigh
+    )
 
     def two_ticks(first, outs, *args):
         scratch = [VM(*full(UNITS)), VM((2, 2, ROWS, COLS), f32), VM((2, 2, ROWS, COLS), f32)]
@@ -544,6 +551,9 @@
     mats = (bhi, blo, shi, slo, trans, refl, strans, srefl)
     x = two_ticks(True, [full(UNITS)], *mats, trans, w, low, high, hlow, hhigh)[0]
     htop, hbot = both_ways(x, x, "tx")
+    wide = call(wide_body, [((2, 2, 128, 192), bf16)], [SM] * 3 + [pl.ANY], flops=1 << 24)(
+        tap_index, tap_other, bank, x
+    )[0]
     tall = ((8, 64, COLS), f32)
     tall_t, tall_r = call(taller_body, [tall] * 2, [SM] + [VM] * 4, flops=1 << 25)(
         media_table, trans, refl, utop, ubot
@@ -557,7 +567,14 @@
     hlow, hhigh = both_ways(low, high, "ty")
     top, bot = two_ticks(False, [half(UNITS)] * 2, *mats, const, w, low, high, hlow, hhigh)
     htop, hbot = both_ways(top, bot, "tx")
-    down, up = call(last_body, [full(UNITS)] * 2, [VM] * 8, flops=1 << 27)(
+    down, up = call(
+        last_body,
+        [full(UNITS)] * 2,
+        [VM] * 8,
+        flops=1 << 27,
+        scratch=[VM(*full(UNITS)), VM(*full(UNITS)), pltpu.SemaphoreType.DMA((UNITS,))],
+        home=pl.ANY,
+    )(
         amat, refl, const, incident, top, bot, htop, hbot
     )
     return down[None], up[None]

time: 73.2 us -> 68.7 us (0.939)
  waiting for transfers between devices: 20.4 us -> 17.3 us
  Pallas kernels: 23 us -> 21.8 us
    ppermute x1, waiting for transfers between devices: 2.26 us -> 0.01 us  [on_device(): note = lax.ppermute(note, 'depth', [(0, 1), (1, 0)])]
    pallas_call x1, Pallas kernels: 1.89 us -> 0.88 us  [on_device(): call(inc_row_body, [((UNITS, 2, 2, 64, COLS), f32)], [VM] * 5, flops=1 <<...]
    ppermute x14, waiting for transfers between devices: 18.1 us -> 17.3 us  [both_ways(): return (lax.ppermute(high, axis, up), lax.ppermute(low, axis, back))]
    pallas_call x2 -> x4, Pallas kernels: 6.91 us -> 6.72 us  [the longest x1 2.57 us: on_device(): call(own_body, lookups(1) + [((384, 128), bf16)] * 2, [SM] * 3 + [VM], fl...]
  transfers between devices with their start and end apart: 15 -> 15, of which waited for: 6 -> 5; matrix products, arithmetic and copies ran while one was open for 0% -> 0% of each run, Pallas kernels for 18% -> 19%
where the time goes in v1:
time: 68.7 us; the launch traced here: 67.4 us
  starting transfers between devices  25.3 us (37%)
  Pallas kernels  21.8 us (32%)
  waiting for transfers between devices  17.3 us (25%)
  local copies, waits for them, and re-layouts  2.1 us (3%)
  between operations  1 us (1%)
    ppermute x14, starting transfers between devices, both_ways(): return (lax.ppermute(high, axis, up), lax.ppermute(low, axis, back))  22.2 us
    ppermute x14, waiting for transfers between devices, both_ways(): return (lax.ppermute(high, axis, up), lax.ppermute(low, axis, back))  17.3 us
    pallas_call x2, Pallas kernels, two_ticks(): call(functools.partial(column_body, first), outs, [VM] * len(args), flops...  5.6 us
    ppermute x1, starting transfers between devices, on_device(): note = lax.ppermute(note, 'depth', [(0, 1), (1, 0)])  3.11 us
    pallas_call x1, Pallas kernels, on_device(): call(second_body, [full(UNITS)] + [packs(3, UNITS)] * 2, [VM] * 7, flops=...  2.9 us
    pallas_call x1, Pallas kernels, on_device(): call(own_body, lookups(1) + [((384, 128), bf16)] * 2, [SM] * 3 + [VM], fl...  2.57 us
    unnamed x14, local copies, waits for them, and re-layouts  2.1 us
    pallas_call x1, Pallas kernels, on_device(): call(row_body, [full(16)] + [packs(2, 16)] * 2, [VM] * 5, flops=1 << 27)  1.98 us
  transfers between devices with their start and end apart: 15, of which 5 were waited for; matrix products, arithmetic and copies ran while one was open for 0% of the time, Pallas kernels for 19%

profile of v1, /device:TPU:24, one launch (start us, length us, event | category | flops | bytes accessed | tf_op | source)
XLA Modules:
  0.0 67.4 jit_solution(1379633449358901618)
XLA Ops:
  0.6 1.0 %copy-done.1 = f32[1,8,2,2,32,128]{5,4,3,2,1,0:T(8,128)S(1)} copy-done((f32[1,8,2,2,32,128]{5,4,3,2,1,0:T(8,128)S(1)}, f32[1,8,2,2,32,128]{5,4,3,2,1,0:T(8,128)}, u32[]{:S(2)}) %copy-start.1) | copy-done | bytes 524312
  1.7 1.0 %copy-done.2 = f32[1,8,2,2,32,128]{5,4,3,2,1,0:T(8,128)S(1)} copy-done((f32[1,8,2,2,32,128]{5,4,3,2,1,0:T(8,128)S(1)}, f32[1,8,2,2,32,128]{5,4,3,2,1,0:T(8,128)}, u32[]{:S(2)}) %copy-start.2) | copy-done | bytes 524312
  2.8 5.3 %collective-permute-start.1 = (f32[16,2,2,16,128]{4,3,2,1,0:T(8,128)S(1)}, f32[16,2,2,16,128]{4,3,2,1,0:T(8,128)S(1)}, u32[]{:S(2)}, u32[]{:S(2)}) collective-permute-start(f32[16,2,2,16,128]{4,3,2,1,0:T(8,128)S(1)} %get-tuple-element.43.top), channel_id=1, source_target_pairs={{8,0},{16,8},{24,16},{32,24},{40,32},{48,40},{56,48},{64,56},{72,6... | collective-permute-start | bytes 1572872 | tf_op jit(solution)/shard_map/ppermute | solution.py:496
  8.7 1.2 %collective-permute-start.2 = (f32[5,32,128]{2,1,0:T(8,128)S(1)}, f32[5,32,128]{2,1,0:T(8,128)S(1)}, u32[]{:S(2)}, u32[]{:S(2)}) collective-permute-start(f32[5,32,128]{2,1,0:T(8,128)S(1)} %get-tuple-element.45), channel_id=1, source_target_pairs={{0,1},{1,2},{2,3},{3,4},{4,5},{5,6},{6,7},{7,0},{8,9},{9,10},{10,1... | collective-permute-start | bytes 245768 | tf_op jit(solution)/shard_map/ppermute | solution.py:496
  10.8 3.1 %collective-permute-start.4 = (s32[40,128]{1,0:T(8,128)S(1)}, s32[40,128]{1,0:T(8,128)S(1)}, u32[]{:S(2)}, u32[]{:S(2)}) collective-permute-start(s32[40,128]{1,0:T(8,128)S(1)} %pad_add_fusion), channel_id=1, source_target_pairs={{0,128},{128,0},{1,129},{129,1},{2,130},{130,2},{3,131},{131,3},{4... | collective-permute-start | bytes 61448 | tf_op jit(solution)/shard_map/ppermute | solution.py:521
  13.9 2.6 %shard_map.86 = (bf16[1,128,256]{2,1,0:T(8,128)(2,1)S(1)}, bf16[1,384,256]{2,1,0:T(8,128)(2,1)S(1)}, bf16[1,384,256]{2,1,0:T(8,128)(2,1)S(1)}, f32[1,8,32,128]{3...) custom-call(s32[1,2]{1,0:T(1,128)S(1)} %copy-done.6, ...), custom_call_target="tpu_custom_call" | custom-call | flops 134217728 | tf_op jit(solution)/shard_map/pallas_call | solution.py:526
  16.5 2.0 %shard_map.89 = (f32[16,2,2,32,128]{4,3,2,1,0:T(8,128)S(1)}, f32[2,4,2,32,128]{4,3,2,1,0:T(8,128)S(1)}, f32[2,4,2,32,128]{4,3,2,1,0:T(8,128)S(1)}) custom-call(bf16[1,128,256]{2,1,0:T(8,128)(2,1)S(1)} %get-tuple-element.42.amat.refs_0_, f32[16,2,2,16,128]{4,3,2,1,0:T(8,128)S(1)} %get-tuple-element.43.top, f32[16,2,2,16,128]{4,3,2,1,0:T(8,128)S(1)} %get-tuple-element.44.bot, ...), custom_call_target="tpu_custom_call" | custom-call | flops 134217728 | tf_op jit(solution)/shard_map/pallas_call | solution.py:530
  18.5 3.0 %collective-permute-start.5 = (f32[2,4,2,32,128]{4,3,2,1,0:T(8,128)S(1)}, f32[2,4,2,32,128]{4,3,2,1,0:T(8,128)S(1)}, u32[]{:S(2)}, u32[]{:S(2)}) collective-permute-start(f32[2,4,2,32,128]{4,3,2,1,0:T(8,128)S(1)} %get-tuple-element.72.high), channel_id=1, source_target_pairs={{0,1},{1,2},{2,3},{3,4},{4,5},{5,6},{6,7},{7,0},{8,9},{9,10},{10,1... | collective-permute-start | bytes 786440 | tf_op jit(solution)/shard_map/ppermute | solution.py:496
  21.5 1.8 %shard_map.90 = (bf16[2,128,256]{2,1,0:T(8,128)(2,1)S(1)}, bf16[2,384,256]{2,1,0:T(8,128)(2,1)S(1)}, bf16[2,384,256]{2,1,0:T(8,128)(2,1)S(1)}, f32[2,8,32,128]{3,2,1,0:T(8,128)S(1)}, f32[2,8,32,128]{3,2,1,0:T(8,128)S(1)}) custom-call(s32[1,2]{1,0:T(1,128)S(1)} %slice.6.tap.tap_other, f32[16,33]{1,0:T(8,128)S(1)} %bitcast.12, f32[16,16]{1,0:T(8,128)S(1)} %copy-done.3, ...), custom_call_target="tpu_custom_call" | custom-call | flops 67108864 | tf_op jit(solution)/shard_map/pallas_call | solution.py:536
  24.2 2.9 %collective-permute-start.8 = (f32[33,32,128]{2,1,0:T(8,128)S(1)}, f32[33,32,128]{2,1,0:T(8,128)S(1)}, u32[]{:S(2)}, u32[]{:S(2)}) collective-permute-start(f32[33,32,128]{2,1,0:T(8,128)S(1)} %shard_map.94.x), channel_id=1, source_target_pairs={{8,0},{16,8},{24,16},{32,24},{40,32},{48,40},{56,48},{64,56},{72,6... | collective-permute-start | bytes 1622024 | tf_op jit(solution)/shard_map/ppermute | solution.py:496
  27.1 1.3 %shard_map.91 = (f32[2,8,32,128]{3,2,1,0:T(8,128)S(1)}, f32[2,8,32,128]{3,2,1,0:T(8,128)S(1)}) custom-call(f32[16,16]{1,0:T(8,128)S(1)} %copy-done.3, f32[5,32,128]{2,1,0:T(8,128)S(1)} %collective-permute-done.2.elow, f32[5,32,128]{2,1,0:T(8,128)S(1)} %collective-permute-done.3.ehigh), custom_call_target="tpu_custom_call" | custom-call | flops 33554432 | tf_op jit(solution)/shard_map/pallas_call | solution.py:543
  28.4 1.6 %collective-permute-done.6.hhigh = f32[2,4,2,32,128]{4,3,2,1,0:T(8,128)S(1)} collective-permute-done((f32[2,4,2,32,128]{4,3,2,1,0:T(8,128)S(1)}, f32[2,4,2,32,128]{4,3,2,1,0:T(8,128)S(1)}, u32[]{:S(2)}, u32[]{:S(2)}) %collective-permute-start.6) | collective-permute-done | bytes 262176 | tf_op jit(solution)/shard_map/ppermute | solution.py:496
  30.0 3.1 %shard_map.92.x = f32[8,2,2,32,128]{4,3,2,1,0:T(8,128)S(1)} custom-call(bf16[2,384,256]{2,1,0:T(8,128)(2,1)S(1)} %get-tuple-element.61.bhi, bf16[2,384,256]{2,1,0:T(8,128)(2,1)S(1)} %get-tuple-element.62.blo, bf16[384,128]{1,0:T(8,128)(2,1)S(1)} %get-tuple-element.63.shi, bf16[384,128]{1,0:T(8,128)(2,1)S(1)} %get-tuple-element.64.slo, ...), custom_call_target="tpu_custom_call" | custom-call | flops 134217728 | tf_op jit(solution)/shard_map/pallas_call | solution.py:549
  33.1 2.9 %collective-permute-start.10 = (f32[8,2,2,32,128]{4,3,2,1,0:T(8,128)S(1)}, f32[8,2,2,32,128]{4,3,2,1,0:T(8,128)S(1)}, u32[]{:S(2)}, u32[]{:S(2)}) collective-permute-start(f32[8,2,2,32,128]{4,3,2,1,0:T(8,128)S(1)} %shard_map.92.x), channel_id=1, source_target_pairs={{8,0},{16,8},{24,16},{32,24},{40,32},{48,40},{56,48},{64,56},{72,6... | collective-permute-start | bytes 1572872 | tf_op jit(solution)/shard_map/ppermute | solution.py:496
  36.1 1.1 %shard_map.93.wide = bf16[2,2,128,192]{3,2,1,0:T(8,128)(2,1)S(1)} custom-call(s32[1,2]{1,0:T(1,128)S(1)} %copy-done.6, s32[1,2]{1,0:T(1,128)S(1)} %slice.6.tap.tap_other, f32[16,33]{1,0:T(8,128)S(1)} %bitcast.13, f32[8,2,2,32,128]{4,3,2,1,0:T(8,128)S(1)} %shard_map.92.x), custom_call_target="tpu_custom_call" | custom-call | flops 16777216 | tf_op jit(solution)/shard_map/pallas_call | solution.py:554
  39.0 3.9 %collective-permute-done.9.htop = f32[8,2,2,32,128]{4,3,2,1,0:T(8,128)S(1)} collective-permute-done((f32[8,2,2,32,128]{4,3,2,1,0:T(8,128)S(1)}, f32[8,2,2,32,128]{4,3,2,1,0:T(8,128)S(1)}, u32[]{:S(2)}, u32[]{:S(2)}) %collective-permute-start.9) | collective-permute-done | bytes 524320 | tf_op jit(solution)/shard_map/ppermute | solution.py:496
  42.9 2.9 %shard_map.97 = (f32[8,2,2,32,128]{4,3,2,1,0:T(8,128)S(1)}, f32[3,2,2,32,128]{4,3,2,1,0:T(8,128)S(1)}, f32[3,2,2,32,128]{4,3,2,1,0:T(8,128)S(1)}) custom-call(bf16[2,128,256]{2,1,0:T(8,128)(2,1)S(1)} %get-tuple-element.59.amat, bf16[2,2,128,192]{3,2,1,0:T(8,128)(2,1)S(1)} %shard_map.93.wide, f32[8,64,128]{2,1,0:T(8,128)S(1)} %get-tuple-element.74.tall_r, ...), custom_call_target="tpu_custom_call" | custom-call | flops 134217728 | tf_op jit(solution)/shard_map/pallas_call | solution.py:564
  45.8 2.9 %collective-permute-start.11 = (f32[3,2,2,32,128]{4,3,2,1,0:T(8,128)S(1)}, f32[3,2,2,32,128]{4,3,2,1,0:T(8,128)S(1)}, u32[]{:S(2)}, u32[]{:S(2)}) collective-permute-start(f32[3,2,2,32,128]{4,3,2,1,0:T(8,128)S(1)} %get-tuple-element.77.high), channel_id=1, source_target_pairs={{0,1},{1,2},{2,3},{3,4},{4,5},{5,6},{6,7},{7,0},{8,9},{9,10},{10,1... | collective-permute-start | bytes 589832 | tf_op jit(solution)/shard_map/ppermute | solution.py:496
  48.7 3.2 %collective-permute-done.11.hlow = f32[3,2,2,32,128]{4,3,2,1,0:T(8,128)S(1)} collective-permute-done((f32[3,2,2,32,128]{4,3,2,1,0:T(8,128)S(1)}, f32[3,2,2,32,128]{4,3,2,1,0:T(8,128)S(1)}, u32[]{:S(2)}, u32[]{:S(2)}) %collective-permute-start.11) | collective-permute-done | bytes 196640 | tf_op jit(solution)/shard_map/ppermute | solution.py:496
  51.9 4.6 %collective-permute-done.12.hhigh = f32[3,2,2,32,128]{4,3,2,1,0:T(8,128)S(1)} collective-permute-done((f32[3,2,2,32,128]{4,3,2,1,0:T(8,128)S(1)}, f32[3,2,2,32,128]{4,3,2,1,0:T(8,128)S(1)}, u32[]{:S(2)}, u32[]{:S(2)}) %collective-permute-start.12) | collective-permute-done | bytes 196640 | tf_op jit(solution)/shard_map/ppermute | solution.py:496
  56.5 2.5 %shard_map.98 = (f32[8,2,2,16,128]{4,3,2,1,0:T(8,128)S(1)}, f32[8,2,2,16,128]{4,3,2,1,0:T(8,128)S(1)}) custom-call(bf16[2,384,256]{2,1,0:T(8,128)(2,1)S(1)} %get-tuple-element.61.bhi, bf16[2,384,256]{2,1,0:T(8,128)(2,1)S(1)} %get-tuple-element.62.blo, bf16[384,128]{1,0:T(8,128)(2,1)S(1)} %get-tuple-element.63.shi, ...), custom_call_target="tpu_custom_call" | custom-call | flops 134217728 | tf_op jit(solution)/shard_map/pallas_call | solution.py:549
  59.0 2.9 %collective-permute-start.14 = (f32[8,2,2,16,128]{4,3,2,1,0:T(8,128)S(1)}, f32[8,2,2,16,128]{4,3,2,1,0:T(8,128)S(1)}, u32[]{:S(2)}, u32[]{:S(2)}) collective-permute-start(f32[8,2,2,16,128]{4,3,2,1,0:T(8,128)S(1)} %get-tuple-element.78.top), channel_id=1, source_target_pairs={{8,0},{16,8},{24,16},{32,24},{40,32},{48,40},{56,48},{64,56},{72,6... | collective-permute-start | bytes 786440 | tf_op jit(solution)/shard_map/ppermute | solution.py:496
  61.9 4.1 %collective-permute-done.13.htop = f32[8,2,2,16,128]{4,3,2,1,0:T(8,128)S(1)} collective-permute-done((f32[8,2,2,16,128]{4,3,2,1,0:T(8,128)S(1)}, f32[8,2,2,16,128]{4,3,2,1,0:T(8,128)S(1)}, u32[]{:S(2)}, u32[]{:S(2)}) %collective-permute-start.13) | collective-permute-done | bytes 262176 | tf_op jit(solution)/shard_map/ppermute | solution.py:496
  66.0 1.3 %shard_map.99 = (f32[8,2,2,32,128]{4,3,2,1,0:T(8,128)}, f32[8,2,2,32,128]{4,3,2,1,0:T(8,128)}) custom-call(bf16[2,128,256]{2,1,0:T(8,128)(2,1)S(1)} %get-tuple-element.59.amat, f32[2,8,32,128]{3,2,1,0:T(8,128)S(1)} %get-tuple-element.60.refl, f32[8,2,2,64,128]{4,3,2,1,0:T(8,128)S(1)} %shard_map.96.const, f32[8,2,2,32,128]{4,3,2,1,0:T(8,128)S(1)} %copy-done, ...), custom_call_target="tpu_custom_call" | custom-call | flops 134217728 | tf_op jit(solution)/shard_map/pallas_call | solution.py:570
  (37 shorter events, 4.3 us)
Async XLA Ops:
  0.6 1.0 %copy-start.1 = (f32[1,8,2,2,32,128]{5,4,3,2,1,0:T(8,128)S(1)}, f32[1,8,2,2,32,128]{5,4,3,2,1,0:T(8,128)}, u32[]{:S(2)}) copy-start(f32[1,8,2,2,32,128]{5,4,3,2,1,0:T(8,128)} %param.7) | copy-start | bytes 1572868
  1.7 1.0 %copy-start.2 = (f32[1,8,2,2,32,128]{5,4,3,2,1,0:T(8,128)S(1)}, f32[1,8,2,2,32,128]{5,4,3,2,1,0:T(8,128)}, u32[]{:S(2)}) copy-start(f32[1,8,2,2,32,128]{5,4,3,2,1,0:T(8,128)} %param.8) | copy-start | bytes 1572868
  2.7 5.4 %copy-start = (f32[8,2,2,32,128]{4,3,2,1,0:T(8,128)S(1)}, f32[8,2,2,32,128]{4,3,2,1,0:T(8,128)}, u32[]{:S(2)}) copy-start(f32[8,2,2,32,128]{4,3,2,1,0:T(8,128)} %inc.5) | copy-start | bytes 1572868
  2.7 5.4 %copy-start.4 = (s32[1,32,128]{2,1,0:T(8,128)S(1)}, s32[1,32,128]{2,1,0:T(8,128)}, u32[]{:S(2)}) copy-start(s32[1,32,128]{2,1,0:T(8,128)} %param.10) | copy-start | bytes 49156
  2.8 13.7 %collective-permute-start = (f32[16,2,2,16,128]{4,3,2,1,0:T(8,128)S(1)}, f32[16,2,2,16,128]{4,3,2,1,0:T(8,128)S(1)}, u32[]{:S(2)}, u32[]{:S(2)}) collective-permute-start(f32[16,2,2,16,128]{4,3,2,1,0:T(8,128)S(1)} %get-tuple-element.44.bot), channel_id=1, source_target_pairs={{0,8},{8,16},{16,24},{24,32},{32,40},{40,48},{48,56},{56,64},{64,7... | collective-permute-start | bytes 1572872 | tf_op jit(solution)/shard_map/ppermute | solution.py:496
  2.8 13.7 %collective-permute-start.1 = (f32[16,2,2,16,128]{4,3,2,1,0:T(8,128)S(1)}, f32[16,2,2,16,128]{4,3,2,1,0:T(8,128)S(1)}, u32[]{:S(2)}, u32[]{:S(2)}) collective-permute-start(f32[16,2,2,16,128]{4,3,2,1,0:T(8,128)S(1)} %get-tuple-element.43.top), channel_id=1, source_target_pairs={{8,0},{16,8},{24,16},{32,24},{40,32},{48,40},{56,48},{64,56},{72,6... | collective-permute-start | bytes 1572872 | tf_op jit(solution)/shard_map/ppermute | solution.py:496
  8.6 2.1 %copy-start.6 = (s32[1,2]{1,0:T(1,128)S(1)}, s32[1,2]{1,0:T(1,128)}, u32[]{:S(2)}) copy-start(s32[1,2]{1,0:T(1,128)} %tap_own.1) | copy-start | bytes 28
  8.7 7.8 %collective-permute-start.2 = (f32[5,32,128]{2,1,0:T(8,128)S(1)}, f32[5,32,128]{2,1,0:T(8,128)S(1)}, u32[]{:S(2)}, u32[]{:S(2)}) collective-permute-start(f32[5,32,128]{2,1,0:T(8,128)S(1)} %get-tuple-element.45), channel_id=1, source_target_pairs={{0,1},{1,2},{2,3},{3,4},{4,5},{5,6},{6,7},{7,0},{8,9},{9,10},{10,1... | collective-permute-start | bytes 245768 | tf_op jit(solution)/shard_map/ppermute | solution.py:496
  9.9 4.0 %copy-start.3 = (f32[16,16]{1,0:T(8,128)S(1)}, f32[16,16]{1,0:T(8,128)}, u32[]{:S(2)}) copy-start(f32[16,16]{1,0:T(8,128)} %table.7) | copy-start | bytes 3076
  9.9 4.0 %copy-start.5 = (f32[8,2,33]{2,1,0:T(2,128)S(1)}, f32[8,2,33]{2,1,0:T(2,128)}, u32[]{:S(2)}) copy-start(f32[8,2,33]{2,1,0:T(2,128)} %param.13) | copy-start | bytes 6340
  9.9 6.6 %collective-permute-start.3 = (f32[5,32,128]{2,1,0:T(8,128)S(1)}, f32[5,32,128]{2,1,0:T(8,128)S(1)}, u32[]{:S(2)}, u32[]{:S(2)}) collective-permute-start(f32[5,32,128]{2,1,0:T(8,128)S(1)} %get-tuple-element.46), channel_id=1, source_target_pairs={{1,0},{2,1},{3,2},{4,3},{5,4},{6,5},{7,6},{0,7},{9,8},{10,9},{11,1... | collective-permute-start | bytes 245768 | tf_op jit(solution)/shard_map/ppermute | solution.py:496
  10.8 5.7 %collective-permute-start.4 = (s32[40,128]{1,0:T(8,128)S(1)}, s32[40,128]{1,0:T(8,128)S(1)}, u32[]{:S(2)}, u32[]{:S(2)}) collective-permute-start(s32[40,128]{1,0:T(8,128)S(1)} %pad_add_fusion), channel_id=1, source_target_pairs={{0,128},{128,0},{1,129},{129,1},{2,130},{130,2},{3,131},{131,3},{4... | collective-permute-start | bytes 61448 | tf_op jit(solution)/shard_map/ppermute | solution.py:521
  18.5 9.9 %collective-permute-start.5 = (f32[2,4,2,32,128]{4,3,2,1,0:T(8,128)S(1)}, f32[2,4,2,32,128]{4,3,2,1,0:T(8,128)S(1)}, u32[]{:S(2)}, u32[]{:S(2)}) collective-permute-start(f32[2,4,2,32,128]{4,3,2,1,0:T(8,128)S(1)} %get-tuple-element.72.high), channel_id=1, source_target_pairs={{0,1},{1,2},{2,3},{3,4},{4,5},{5,6},{6,7},{7,0},{8,9},{9,10},{10,1... | collective-permute-start | bytes 786440 | tf_op jit(solution)/shard_map/ppermute | solution.py:496
  21.5 8.5 %collective-permute-start.6 = (f32[2,4,2,32,128]{4,3,2,1,0:T(8,128)S(1)}, f32[2,4,2,32,128]{4,3,2,1,0:T(8,128)S(1)}, u32[]{:S(2)}, u32[]{:S(2)}) collective-permute-start(f32[2,4,2,32,128]{4,3,2,1,0:T(8,128)S(1)} %get-tuple-element.71.low), channel_id=1, source_target_pairs={{1,0},{2,1},{3,2},{4,3},{5,4},{6,5},{7,6},{0,7},{9,8},{10,9},{11,1... | collective-permute-start | bytes 786440 | tf_op jit(solution)/shard_map/ppermute | solution.py:496
  24.2 13.0 %collective-permute-start.7 = (f32[33,32,128]{2,1,0:T(8,128)S(1)}, f32[33,32,128]{2,1,0:T(8,128)S(1)}, u32[]{:S(2)}, u32[]{:S(2)}) collective-permute-start(f32[33,32,128]{2,1,0:T(8,128)S(1)} %shard_map.94.x), channel_id=1, source_target_pairs={{0,8},{8,16},{16,24},{24,32},{32,40},{40,48},{48,56},{56,64},{64,7... | collective-permute-start | bytes 1622024 | tf_op jit(solution)/shard_map/ppermute | solution.py:496
  24.2 13.0 %collective-permute-start.8 = (f32[33,32,128]{2,1,0:T(8,128)S(1)}, f32[33,32,128]{2,1,0:T(8,128)S(1)}, u32[]{:S(2)}, u32[]{:S(2)}) collective-permute-start(f32[33,32,128]{2,1,0:T(8,128)S(1)} %shard_map.94.x), channel_id=1, source_target_pairs={{8,0},{16,8},{24,16},{32,24},{40,32},{48,40},{56,48},{64,56},{72,6... | collective-permute-start | bytes 1622024 | tf_op jit(solution)/shard_map/ppermute | solution.py:496
  33.1 9.8 %collective-permute-start.9 = (f32[8,2,2,32,128]{4,3,2,1,0:T(8,128)S(1)}, f32[8,2,2,32,128]{4,3,2,1,0:T(8,128)S(1)}, u32[]{:S(2)}, u32[]{:S(2)}) collective-permute-start(f32[8,2,2,32,128]{4,3,2,1,0:T(8,128)S(1)} %shard_map.92.x), channel_id=1, source_target_pairs={{0,8},{8,16},{16,24},{24,32},{32,40},{40,48},{48,56},{56,64},{64,7... | collective-permute-start | bytes 1572872 | tf_op jit(solution)/shard_map/ppermute | solution.py:496
  33.1 9.8 %collective-permute-start.10 = (f32[8,2,2,32,128]{4,3,2,1,0:T(8,128)S(1)}, f32[8,2,2,32,128]{4,3,2,1,0:T(8,128)S(1)}, u32[]{:S(2)}, u32[]{:S(2)}) collective-permute-start(f32[8,2,2,32,128]{4,3,2,1,0:T(8,128)S(1)} %shard_map.92.x), channel_id=1, source_target_pairs={{8,0},{16,8},{24,16},{32,24},{40,32},{48,40},{56,48},{64,56},{72,6... | collective-permute-start | bytes 1572872 | tf_op jit(solution)/shard_map/ppermute | solution.py:496
  45.8 6.0 %collective-permute-start.11 = (f32[3,2,2,32,128]{4,3,2,1,0:T(8,128)S(1)}, f32[3,2,2,32,128]{4,3,2,1,0:T(8,128)S(1)}, u32[]{:S(2)}, u32[]{:S(2)}) collective-permute-start(f32[3,2,2,32,128]{4,3,2,1,0:T(8,128)S(1)} %get-tuple-element.77.high), channel_id=1, source_target_pairs={{0,1},{1,2},{2,3},{3,4},{4,5},{5,6},{6,7},{7,0},{8,9},{9,10},{10,1... | collective-permute-start | bytes 589832 | tf_op jit(solution)/shard_map/ppermute | solution.py:496
  48.7 7.8 %collective-permute-start.12 = (f32[3,2,2,32,128]{4,3,2,1,0:T(8,128)S(1)}, f32[3,2,2,32,128]{4,3,2,1,0:T(8,128)S(1)}, u32[]{:S(2)}, u32[]{:S(2)}) collective-permute-start(f32[3,2,2,32,128]{4,3,2,1,0:T(8,128)S(1)} %get-tuple-element.76.low), channel_id=1, source_target_pairs={{1,0},{2,1},{3,2},{4,3},{5,4},{6,5},{7,6},{0,7},{9,8},{10,9},{11,1... | collective-permute-start | bytes 589832 | tf_op jit(solution)/shard_map/ppermute | solution.py:496
  59.0 7.0 %collective-permute-start.13 = (f32[8,2,2,16,128]{4,3,2,1,0:T(8,128)S(1)}, f32[8,2,2,16,128]{4,3,2,1,0:T(8,128)S(1)}, u32[]{:S(2)}, u32[]{:S(2)}) collective-permute-start(f32[8,2,2,16,128]{4,3,2,1,0:T(8,128)S(1)} %get-tuple-element.79.bot), channel_id=1, source_target_pairs={{0,8},{8,16},{16,24},{24,32},{32,40},{40,48},{48,56},{56,64},{64,7... | collective-permute-start | bytes 786440 | tf_op jit(solution)/shard_map/ppermute | solution.py:496
  59.0 7.0 %collective-permute-start.14 = (f32[8,2,2,16,128]{4,3,2,1,0:T(8,128)S(1)}, f32[8,2,2,16,128]{4,3,2,1,0:T(8,128)S(1)}, u32[]{:S(2)}, u32[]{:S(2)}) collective-permute-start(f32[8,2,2,16,128]{4,3,2,1,0:T(8,128)S(1)} %get-tuple-element.78.top), channel_id=1, source_target_pairs={{8,0},{16,8},{24,16},{32,24},{40,32},{48,40},{56,48},{64,56},{72,6... | collective-permute-start | bytes 786440 | tf_op jit(solution)/shard_map/ppermute | solution.py:496
